TPU v7x, 32 devices: a whole 2x2x4 slice. The times are simulated.
32 devices in a mesh: grp: 4 (over y, x), clu: 8 (over z, core).
Axes of the slice: x: 2, y: 2, z: 4, core: 2. Of those that a mesh axis runs over, the one named last changes fastest.
Arguments:
- forces: bfloat16 [3, 2048, 512], P(None, 'clu'), may hold values from -6 to 6
- order: int32 [2048], P('clu'), may hold values from 0 to 2047, as said below
- bases: bfloat16 [2, 32, 3, 2048], P(None, None, None, 'clu'), may hold values from -0.21875 to 0.21875
- near_tiles: bfloat16 [8, 8, 768, 768], P('clu', 'grp'), may hold values from -0.078125 to 0.078125
- near_col: int32 [8, 8], P('clu', 'grp'), may hold values from 0 to 7, as said below
- far_basis: bfloat16 [8, 64, 32, 768], P('clu', 'grp'), may hold values from -0.125 to 0.125
- far_coupling: bfloat16 [8, 64, 32, 32], P('clu', 'grp'), may hold values from -1 to 1
- far_scale: float32 [8, 64], P('clu', 'grp'), may hold values from 0.5 to 2
- far_rank: int32 [8, 64], P('clu', 'grp'), may hold values from 8 to 32
- far_target: int32 [8, 64], P('clu', 'grp'), may hold values from 0 to 5, as said below
Outputs:
- velocity: float32 [3, 2048, 512], P(None, 'clu', 'grp')
Inputs may be any that keep to these rules, and one draw needn't show every extreme that they name: `order`: A permutation of the bead numbers; the 256 positions of row block c hold beads of chain blocks c - 1, c and c + 1 only, counted cyclically, exactly 64 of them from chain block c - 1 and exactly 64 from chain block c + 1. `near_col`: each near tile's column block lies within two blocks of its row block, counted cyclically. `far_target`: level l takes indices 2 ** (l + 1) - 2 to 2 ** (l + 2) - 3; the named cluster never contains the block's own row block.
All inputs are finite; a program needn't handle non-finite values.
Results may differ from a plain program's by a relative error of at most 0.0025.
Values may be sent and summed in bfloat16 or wider, within the bound.
A program may use at most 64 MiB of HBM per device.

v0:
```python
import functools

import jax
import jax.numpy as jnp
from jax import lax
from jax.experimental import pallas as pl
from jax.experimental.pallas import tpu as pltpu
from jax.sharding import PartitionSpec as P

MESH = pl.DeviceIdType.MESH
F32, BF16 = jnp.float32, jnp.bfloat16


def kernel(
    n, groups, levels, rank,
    forces, order, bases, tiles_hbm, near_col, basis_hbm, coupling, scale, ranks, targets,
    out,
    raw, ext, ext_out, orders, tiles, basis, spread, picks, own_pick, piece_out, piece_mate, pieces,
    table_out, tables, coupled, total, y_out, y_in,
    local_sem, order_send, order_recv, raw_send, raw_recv, ext_send, ext_recv,
    piece_send, piece_recv, table_send, table_recv, y_send, y_recv,
):
    g, c = lax.axis_index("grp"), lax.axis_index("clu")
    core = lax.rem(c, 2)
    comps, tile, columns = forces.shape
    width = columns // groups
    quarter = tile // 4
    slots = raw.shape[1]
    rows = comps * tile
    near_count = tiles.shape[0]
    far_count = targets.shape[1]
    coarse = 2 ** (levels + 1) - 2
    half = n // 2

    def at_clu(by):
        return {"grp": g, "clu": lax.rem(c + by + n, n)}

    partners = (g, g + 1 - 2 * lax.rem(g, 2), lax.rem(g + 2, groups), groups - 1 - g)

    def at_grp(i):
        return {"grp": partners[i], "clu": c}

    mate = {"grp": g, "clu": c + 1 - 2 * core}

    def remote(src, dst, send, recv, where):
        return pltpu.make_async_remote_copy(
            src_ref=src, dst_ref=dst, send_sem=send, recv_sem=recv, device_id=where, device_id_type=MESH
        )

    def own_columns(i):
        q = partners[i]
        return forces.at[:, :, pl.ds(pl.multiple_of(q * width, width), width)]

    local = [pltpu.make_async_copy(own_columns(i), raw.at[i, 2 + core], local_sem.at[i]) for i in range(groups)]
    for copy in local:
        copy.start()
    tiles_copy = pltpu.make_async_copy(tiles_hbm, tiles, local_sem.at[groups])
    basis_copy = pltpu.make_async_copy(basis_hbm, basis, local_sem.at[groups + 1])
    tiles_copy.start()
    basis_copy.start()

    barrier = pltpu.get_barrier_semaphore()

    def greet(d, carry):
        pl.semaphore_signal(barrier, inc=1, device_id=at_clu(d), device_id_type=MESH)
        return carry

    lax.fori_loop(1, n, greet, 0)
    for d in range(1, groups):
        pl.semaphore_signal(barrier, inc=1, device_id=at_grp(d), device_id_type=MESH)
    pl.semaphore_wait(barrier, n - 1 + groups - 1)

    sends = []
    near_groups, far_group = range(1, groups - 1), groups - 1
    offsets = (-2, -1, 1, 2)
    order_copies = []
    for at, by in enumerate(offsets):
        copy = remote(order, orders.at[2 - by], order_send.at[at], order_recv.at[2 - by], at_clu(by))
        copy.start()
        order_copies.append(copy)

    def send_raw(i):
        group = [
            remote(own_columns(i), raw.at[i, core], raw_send.at[i, 0], raw_recv.at[i, core], at_clu(2)),
            remote(own_columns(i), raw.at[i, 4 + core], raw_send.at[i, 1], raw_recv.at[i, 4 + core], at_clu(-2)),
        ]
        for copy in group:
            copy.start()
            sends.append(copy)

    def send_mate(i):
        copy = remote(own_columns(i), raw.at[i, 2 + core], raw_send.at[i, 2], raw_recv.at[i, 2 + core], mate)
        copy.start()
        sends.append(copy)

    def arrived(i, slot):
        remote(raw.at[i, slot], raw.at[i, slot], raw_send.at[i, 0], raw_recv.at[i, slot], mate).wait_recv()

    def take_raw(i):
        for at, slot in ((3, core), (4, 4 + core)):
            arrived(i, slot)
            if i == 0:
                for to in near_groups:
                    across = remote(
                        raw.at[0, slot], raw.at[to, slot], raw_send.at[to, at - 3], raw_recv.at[to, slot], at_grp(to)
                    )
                    across.start()
                    sends.append(across)
            copy = remote(raw.at[i, slot], raw.at[i, slot], raw_send.at[i, at], raw_recv.at[i, slot], mate)
            copy.start()
            sends.append(copy)
        for slot in (3 - core, 1 - core, 5 - core):
            arrived(i, slot)

    send_raw(0)
    for i in range(groups):
        send_mate(i)

    lane = lax.broadcasted_iota(jnp.int32, (rank, coarse * rank), 1)
    row = lax.broadcasted_iota(jnp.int32, (rank, coarse * rank), 0)
    repeat = (lax.rem(lane, rank) == row).astype(BF16)
    wide = jnp.dot(coupling[...], repeat, preferred_element_type=F32)
    for b in range(far_count):
        start = targets[0, b] * rank
        keep = (lane >= start) & (lane < start + ranks[0, b])
        spread[b * rank:(b + 1) * rank, :] = jnp.where(keep, wide[b * rank:(b + 1) * rank, :], 0.0).astype(BF16)
    ext[:, quarter:, :] = jnp.zeros((groups, ext.shape[1] - quarter, ext.shape[2]), BF16)

    sub = lax.broadcasted_iota(jnp.int32, (tile, tile), 0)
    lan = lax.broadcasted_iota(jnp.int32, (tile, tile), 1)
    upto = (sub <= lan).astype(BF16)
    first = (c - core - 2) * tile

    def ranked(chosen):
        spots = jnp.broadcast_to(chosen.astype(F32), (8, tile)).astype(BF16)
        return (jnp.dot(spots, upto, preferred_element_type=F32)[0:1, :] - 1.0).astype(jnp.int32)

    def one_hot(cluster_order, dst):
        spot = cluster_order - first
        spot = jnp.where(spot < 0, spot + n * tile, spot)
        spot = jnp.where(spot >= n * tile, spot - n * tile, spot)
        beyond = spot >= slots * tile
        spot = jnp.where(beyond, slots * tile + ranked(beyond), spot)
        down = jnp.broadcast_to(spot.astype(F32), (128, tile)).T
        at = lax.broadcasted_iota(jnp.int32, (tile, 128), 1).astype(F32)
        for j in range(dst.shape[1] // 128):
            dst[:, j * 128:(j + 1) * 128] = (down == at + float(j * 128)).astype(F32).astype(BF16)

    one_hot(order[...], own_pick)
    for copy in local:
        copy.wait()
    for at, by in enumerate(offsets):
        order_copies[at].wait_send()
        remote(orders.at[2 + by], orders.at[2 + by], order_send.at[at], order_recv.at[2 + by], mate).wait_recv()
    orders[2] = order[...]

    away = orders[1 + 2 * core] - c * tile
    chosen = (away >= 0) & (away < tile)
    place = jnp.where(chosen, ranked(chosen), -1)
    left = (lax.broadcasted_iota(jnp.int32, (ext.shape[1], tile), 0) == place).astype(F32).astype(BF16)
    right = (sub == away).astype(F32).astype(BF16)
    pick = lax.dot_general(left, right, (((1,), (1,)), ((), ())), preferred_element_type=F32).astype(BF16)
    for at, i in enumerate((0, far_group)):
        block = jnp.concatenate([raw[i, 2 + core, d] for d in range(comps)], axis=1)
        ext_out[at] = jnp.dot(pick, block, preferred_element_type=F32).astype(BF16)[:quarter]
        copy = remote(
            ext_out.at[at], ext.at[i, 0:quarter], ext_send.at[i], ext_recv.at[i], at_clu(6 * core - 3)
        )
        copy.start()
        sends.append(copy)

    def take_ext(i):
        rows_in = ext.at[i, 0:quarter]
        remote(rows_in, rows_in, ext_send.at[i], ext_recv.at[i], mate).wait_recv()

    def gathered(pick_ref, i, with_ext):
        block = jnp.concatenate([raw[i, :, d].reshape(slots * tile, width) for d in range(comps)], axis=1)
        x = jnp.dot(pick_ref[:, :slots * tile], block, preferred_element_type=F32)
        if with_ext:
            x = x + jnp.dot(
                pick_ref[:, slots * tile:], ext[i], preferred_element_type=F32
            )
        x = x.astype(BF16)
        return jnp.concatenate([x[:, d * width:(d + 1) * width] for d in range(comps)], axis=0)

    take_raw(0)
    own_rows = gathered(own_pick, 0, False)
    piece = jnp.zeros((levels * rank, width), F32)
    for d in range(comps):
        part = jnp.concatenate([bases[level, d] for level in range(levels)], axis=0)
        piece = piece + jnp.dot(part, own_rows[d * tile:(d + 1) * tile], preferred_element_type=F32)
    piece_out[0] = piece
    copy = remote(piece_out.at[0], piece_mate, piece_send.at[0], piece_recv.at[half], mate)
    copy.start()
    sends.append(copy)
    copy.wait_recv()
    pair = piece + piece_mate[...]
    piece_out[1] = pair
    pieces[c // 2] = pair

    def piece_copy(d):
        return remote(piece_out.at[1], pieces.at[c // 2], piece_send.at[d], piece_recv.at[c // 2], at_clu(2 * d))

    def start_piece(d, carry):
        piece_copy(d).start()
        return carry

    lax.fori_loop(1, half, start_piece, 0)
    send_raw(far_group)

    for j in range(near_count):
        spot = near_col[0, j] - c + 2
        spot = jnp.where(spot < 0, spot + n, spot)
        spot = jnp.where(spot >= n, spot - n, spot)
        one_hot(orders[jnp.clip(spot, 0, 4)], picks.at[j])
    tiles_copy.wait()
    basis_copy.wait()

    def near(i):
        part = jnp.zeros((rows, width), F32)
        for j in range(near_count):
            part = part + jnp.dot(tiles[j], gathered(picks.at[j], i, True), preferred_element_type=F32)
        total[i] = part

    def send_y(i):
        y_out[i] = total[i].astype(BF16)
        copy = remote(y_out.at[i], y_in.at[i], y_send.at[i], y_recv.at[i], at_grp(i))
        copy.start()
        sends.append(copy)

    take_ext(0)
    for to in near_groups:
        across = remote(
            ext.at[0, 0:quarter], ext.at[to, 0:quarter], ext_send.at[to], ext_recv.at[to], at_grp(to)
        )
        across.start()
        sends.append(across)

    def await_piece(d, carry):
        source = lax.rem(c // 2 + d, half)
        remote(piece_out.at[1], pieces.at[source], piece_send.at[d], piece_recv.at[source], mate).wait_recv()
        return carry

    lax.fori_loop(1, half, await_piece, 0)
    for level in range(levels):
        count = 2 ** (level + 1)
        members = half // count
        for k in range(count):
            entry = lax.fori_loop(
                0, members,
                lambda m, acc, k=k, members=members, level=level: acc
                + pieces[k * members + m, level * rank:(level + 1) * rank, :],
                jnp.zeros((rank, width), F32),
            )
            at = (count - 2 + k) * rank
            table_out[at:at + rank, :] = entry
            tables[0, at:at + rank, :] = entry
    for d in range(1, groups):
        copy = remote(table_out, tables.at[d], table_send.at[d], table_recv.at[d], at_grp(d))
        copy.start()
        sends.append(copy)
    near(0)
    for i in near_groups:
        take_raw(i)
        take_ext(i)
        near(i)

    for d in range(1, groups):
        remote(table_out, tables.at[d], table_send.at[d], table_recv.at[d], at_grp(d)).wait_recv()
    table = jnp.concatenate([tables[i] for i in range(groups)], axis=1)
    high = table.astype(BF16)
    low = (table - high.astype(F32)).astype(BF16)
    mixed = jnp.dot(spread[...], high, preferred_element_type=F32)
    mixed = mixed + jnp.dot(spread[...], low, preferred_element_type=F32)
    for b in range(far_count):
        coupled[b * rank:(b + 1) * rank, :] = (mixed[b * rank:(b + 1) * rank, :] * scale[0, b]).astype(BF16)
    far = lax.dot_general(basis[...], coupled[...], (((0,), (0,)), ((), ())), preferred_element_type=F32)
    for i in range(groups - 1):
        total[i] = total[i] + far[:, i * width:(i + 1) * width]
    total[groups - 1] = far[:, (groups - 1) * width:]
    for i in range(1, groups - 1):
        send_y(i)
    last = groups - 1
    far_part = total[last]
    take_raw(last)
    take_ext(last)
    near(last)
    total[last] = total[last] + far_part
    send_y(last)

    answer = total[0]
    for i in range(1, groups):
        remote(y_out.at[i], y_in.at[i], y_send.at[i], y_recv.at[i], at_grp(i)).wait_recv()
        answer = answer + y_in[i].astype(F32)
    out[...] = answer.reshape(comps, tile, width)

    for copy in sends:
        copy.wait_send()

    def end_piece(d, carry):
        piece_copy(d).wait_send()
        return carry

    lax.fori_loop(1, half, end_piece, 0)


def solution(mesh):
    n, groups = mesh.shape["clu"], mesh.shape["grp"]

    def on_device(forces, order, bases, near_tiles, near_col, far_basis, far_coupling, far_scale, far_rank, far_target):
        comps, tile, columns = forces.shape
        levels, rank = bases.shape[:2]
        near_count, far_count = near_tiles.shape[1], far_basis.shape[1]
        width, rows, quarter = columns // groups, comps * tile, tile // 4
        coarse = 2 ** (levels + 1) - 2
        slots = 6
        pad = 128
        vmem, smem, hbm = (pl.BlockSpec(memory_space=m) for m in (pltpu.VMEM, pltpu.SMEM, pl.ANY))
        dma = pltpu.SemaphoreType.DMA
        return pl.pallas_call(
            functools.partial(kernel, n, groups, levels, rank),
            out_shape=jax.ShapeDtypeStruct((comps, tile, width), F32),
            in_specs=[hbm, vmem, vmem, hbm, smem, hbm, vmem, smem, smem, smem],
            out_specs=vmem,
            scratch_shapes=[
                pltpu.VMEM((groups, slots, comps, tile, width), BF16),
                pltpu.VMEM((groups, pad, comps * width), BF16),
                pltpu.VMEM((2, quarter, comps * width), BF16),
                pltpu.VMEM((5, 1, tile), jnp.int32),
                pltpu.VMEM((near_count, rows, rows), BF16),
                pltpu.VMEM((far_count * rank, rows), BF16),
                pltpu.VMEM((far_count * rank, coarse * rank), BF16),
                pltpu.VMEM((near_count, tile, slots * tile + pad), BF16),
                pltpu.VMEM((tile, slots * tile), BF16),
                pltpu.VMEM((2, levels * rank, width), F32),
                pltpu.VMEM((levels * rank, width), F32),
                pltpu.VMEM((n // 2, levels * rank, width), F32),
                pltpu.VMEM((coarse * rank, width), F32),
                pltpu.VMEM((groups, coarse * rank, width), F32),
                pltpu.VMEM((far_count * rank, columns), BF16),
                pltpu.VMEM((groups, rows, width), F32),
                pltpu.VMEM((groups, rows, width), BF16),
                pltpu.VMEM((groups, rows, width), BF16),
                dma((groups + 2,)),
                dma((4,)), dma((5,)),
                dma((groups, 5)), dma((groups, slots)),
                dma((groups,)), dma((groups,)),
                dma((n // 2,)), dma((n // 2 + 1,)),
                dma((groups,)), dma((groups,)),
                dma((groups,)), dma((groups,)),
            ],
            compiler_params=pltpu.CompilerParams(
                collective_id=0, has_side_effects=True, vmem_limit_bytes=60 * 1024 * 1024
            ),
        )(
            forces,
            order.reshape(1, tile),
            jnp.transpose(bases, (0, 2, 1, 3)),
            near_tiles.reshape(near_count, rows, rows),
            near_col,
            far_basis.reshape(far_count * rank, rows),
            far_coupling.reshape(far_count * rank, rank),
            far_scale,
            far_rank,
            far_target,
        )

    placed = (
        P(None, "clu", None),
        P("clu"),
        P(None, None, None, "clu"),
        P("clu", "grp", None, None),
        P("clu", "grp"),
        P("clu", "grp", None, None),
        P("clu", "grp", None, None),
        P("clu", "grp"),
        P("clu", "grp"),
        P("clu", "grp"),
    )
    return jax.shard_map(
        on_device, mesh=mesh, in_specs=placed, out_specs=P(None, "clu", "grp"), check_vma=False
    )
```

profile of v0, /device:TPU:0, one launch (start us, length us, event | category | flops | bytes accessed | tf_op | source)
XLA Modules:
  0.0 51.6 jit_solution(14147478873065347541)
XLA Ops:
  0.0 49.9 %shard_map.100 = f32[3,256,128]{2,1,0:T(8,128)} custom-call(bf16[3,256,512]{2,1,0:T(8,128)(2,1)} %forces.1, s32[1,256]{1,0:T(1,128)} %bitcast.9, bf16[2,3,32,256]{3,2,1,0:T(8,128)(2,1)} %bitcast.8, bf16[2,768,768]{2,1,0:T(8,128)(2,1)} %bitcast.5, s32[1,2]{1,0:T(1,128)} %near_col.1, bf16[512,768]{1,0:T(8,128)(2,1)} %bitcast.6, bf16[512,32]{1,0:T(8,128)(2,1)} %bitcast.7, ...), custom_call_target="tpu_custom_call" | custom-call | tf_op jit(solution)/shard_map/pallas_call | solution.py:320
  49.9 1.8 %copy.12 = f32[3,256,128]{2,1,0:T(8,128)} copy(f32[3,256,128]{2,1,0:T(8,128)} %shard_map.100) | data formatting | bytes 786432
where the time goes:
time: 51.8 us; the launch traced here: 51.6 us
  Pallas kernels  49.9 us (96%)
  local copies, waits for them, and re-layouts  1.77 us (3%)
    pallas_call x1, Pallas kernels, on_device(): pl.pallas_call(functools.partial(kernel, n, groups, levels, rank), out_sh...  49.9 us
    unnamed x1, local copies, waits for them, and re-layouts  1.77 us

commit v1 on v0

v1 whole, which is shorter than its diff:
```python
import functools

import jax
import jax.numpy as jnp
from jax import lax
from jax.experimental import pallas as pl
from jax.experimental.pallas import tpu as pltpu
from jax.sharding import PartitionSpec as P

MESH = pl.DeviceIdType.MESH
F32, BF16 = jnp.float32, jnp.bfloat16
SENDS = 112


def kernel(
    n, groups, levels, rank,
    forces, order_hbm, bases_hbm, tiles_hbm, near_col_hbm, basis_hbm, coupling_hbm, scale_hbm, ranks_hbm, targets_hbm,
    out,
    order, bases, coupling, near_col, scale, ranks, targets,
    raw, ext, ext_out, ext_near, orders, tiles, basis, spread, picks, own_pick, piece_out, piece_mate, pieces,
    table_out, tables, coupled, total, y_out, y_in,
    local_sem, own_sem, send_sem, piece_send, order_recv, mate_recv, raw_recv, ext_recv, near_recv,
    pair_recv, piece_recv, table_recv, y_recv,
):
    g, c = lax.axis_index("grp"), lax.axis_index("clu")
    core = lax.rem(c, 2)
    comps, tile, columns = forces.shape
    width = columns // groups
    quarter = tile // 4
    slots = raw.shape[1]
    rows = comps * tile
    near_count = tiles.shape[0]
    far_count = targets.shape[1]
    half = n // 2
    cut = rank // 2
    piece_rows = levels * cut
    blocks = [(level, 2 ** (level + 1)) for level in range(levels)]
    table_rows = sum(count - 1 for _, count in blocks) * cut
    last = groups - 1

    def at_clu(by):
        return {"grp": g, "clu": lax.rem(c + by + n, n)}

    partners = (g, g + 1 - 2 * lax.rem(g, 2), lax.rem(g + 2, groups), groups - 1 - g)

    def at_grp(i):
        return {"grp": partners[i], "clu": c}

    mate = {"grp": g, "clu": c + 1 - 2 * core}
    sends = []

    def remote(src, dst, recv, where, index=0):
        return pltpu.make_async_remote_copy(
            src_ref=src, dst_ref=dst, send_sem=send_sem.at[index], recv_sem=recv, device_id=where, device_id_type=MESH
        )

    def push(src, dst, recv, where):
        assert len(sends) < SENDS
        copy = remote(src, dst, recv, where, len(sends))
        copy.start()
        sends.append(copy)

    def landed(ref, recv):
        remote(ref, ref, recv, mate).wait_recv()

    def columns_of(i, d):
        return forces.at[d, :, pl.ds(pl.multiple_of(partners[i] * width, width), width)]

    def part(i, slot, d):
        return raw.at[i, slot, :, pl.ds(d * width, width)]

    small = [
        pltpu.make_async_copy(src, dst, local_sem.at[at])
        for at, (src, dst) in enumerate((
            (order_hbm, order), (bases_hbm, bases), (near_col_hbm, near_col), (ranks_hbm, ranks),
            (targets_hbm, targets), (scale_hbm, scale), (coupling_hbm, coupling), (basis_hbm, basis), (tiles_hbm, tiles),
        ))
    ]
    for copy in small[:2]:
        copy.start()
    for i in (0, last, 1, 2):
        for d in range(comps):
            pltpu.make_async_copy(columns_of(i, d), part(i, 2 + core, d), own_sem.at[i]).start()
    for copy in small[2:]:
        copy.start()

    barrier = pltpu.get_barrier_semaphore()

    def greet(d, carry):
        pl.semaphore_signal(barrier, inc=1, device_id=at_clu(d), device_id_type=MESH)
        return carry

    lax.fori_loop(1, n, greet, 0)
    for d in range(1, groups):
        pl.semaphore_signal(barrier, inc=1, device_id=at_grp(d), device_id_type=MESH)

    ext[:, quarter:, :] = jnp.zeros((groups, ext.shape[1] - quarter, ext.shape[2]), BF16)
    ext_near[quarter:, :] = jnp.zeros((ext.shape[1] - quarter, ext.shape[2]), BF16)
    small[0].wait()
    pl.semaphore_wait(barrier, n - 1 + groups - 1)

    offsets = (-1, 1, -2, 2)
    for by in offsets:
        push(order, orders.at[2 - by], order_recv.at[2 - by], at_clu(by))

    def send_z(i, d):
        push(columns_of(i, d), part(i, core, d), raw_recv.at[i, core, d], at_clu(2))
        push(columns_of(i, d), part(i, 4 + core, d), raw_recv.at[i, 4 + core, d], at_clu(-2))

    send_z(last, 0)
    for i in (0, last, 1, 2):
        for d in range(comps):
            push(columns_of(i, d), part(i, 2 + core, d), mate_recv.at[i], mate)

    def relay(i, d, across=False):
        for slot in (core, 4 + core):
            landed(part(i, slot, d), raw_recv.at[i, slot, d])
            if across:
                for to, at in ((1, 2), (2, 1)):
                    push(part(i, slot, d), part(at, slot, d), raw_recv.at[at, slot, d], at_grp(to))
            push(part(i, slot, d), part(i, slot, d), raw_recv.at[i, slot, d], mate)

    def take(i, d):
        for slot in (1 - core, 5 - core):
            landed(part(i, slot, d), raw_recv.at[i, slot, d])

    sub = lax.broadcasted_iota(jnp.int32, (tile, tile), 0)
    lan = lax.broadcasted_iota(jnp.int32, (tile, tile), 1)
    upto = (sub <= lan).astype(BF16)

    def ranked(chosen):
        spots = jnp.broadcast_to(chosen.astype(F32), (8, tile)).astype(BF16)
        return (jnp.dot(spots, upto, preferred_element_type=F32)[0:1, :] - 1.0).astype(jnp.int32)

    def one_hot(cluster_order, first, held, dst):
        spot = cluster_order - first * tile
        spot = jnp.where(spot < 0, spot + n * tile, spot)
        spot = jnp.where(spot >= n * tile, spot - n * tile, spot)
        beyond = spot >= held * tile
        spot = jnp.where(beyond, held * tile + ranked(beyond), spot)
        down = jnp.broadcast_to(spot.astype(F32), (128, tile)).T
        at = lax.broadcasted_iota(jnp.int32, (tile, 128), 1).astype(F32)
        for j in range(dst.shape[1] // 128):
            dst[:, j * 128:(j + 1) * 128] = (down == at + float(j * 128)).astype(F32).astype(BF16)

    one_hot(order[...], c - core, 2, own_pick)

    def whole(i, slot):
        return raw.at[i, slot]

    def own_arrived(i):
        pltpu.make_async_copy(whole(i, 2 + core), whole(i, 2 + core), own_sem.at[i]).wait()

    for i in (0, last):
        own_arrived(i)

    def order_landed(by):
        landed(orders.at[2 + by], order_recv.at[2 + by])

    for by in (-1, 1):
        order_landed(by)
    away = orders[1 + 2 * core] - c * tile
    chosen = (away >= 0) & (away < tile)
    place = jnp.where(chosen, ranked(chosen), -1)
    left = (lax.broadcasted_iota(jnp.int32, (ext.shape[1], tile), 0) == place).astype(F32).astype(BF16)
    right = (sub == away).astype(F32).astype(BF16)
    pick = lax.dot_general(left, right, (((1,), (1,)), ((), ())), preferred_element_type=F32).astype(BF16)
    for at, i in enumerate((0, last)):
        ext_out[at] = jnp.dot(pick, raw[i, 2 + core], preferred_element_type=F32).astype(BF16)[:quarter]
        if i == 0:
            push(ext_out.at[0], ext_near.at[0:quarter], near_recv.at[0], at_clu(2 * core - 1))
    send_z(last, 1)

    def ext_in(i):
        return ext.at[i, 0:quarter]

    def send_ext(at, i):
        push(ext_out.at[at], ext_in(i), ext_recv.at[i], at_clu(6 * core - 3))

    send_ext(1, last)

    for copy in small[1:7]:
        copy.wait()
    lane = lax.broadcasted_iota(jnp.int32, (rank, 2 * table_rows), 1)
    row = lax.broadcasted_iota(jnp.int32, (rank, 2 * table_rows), 0)
    lane_row = (lane // table_rows) * cut + lax.rem(lane, cut)
    lane_slot = lax.rem(lane, table_rows) // cut
    repeat = (lane_row == row).astype(F32).astype(BF16)
    wide = jnp.dot(coupling[...], repeat, preferred_element_type=F32)
    for b in range(far_count):
        target = targets[0, b]
        slot_of, base, offset = target, 0, 0
        for level, count in blocks:
            own = (c // 2) // (half // count)
            here = target - base - own - 1
            here = jnp.where(here < 0, here + count, here) + offset
            slot_of = jnp.where((target >= base) & (target < base + count), here, slot_of)
            base, offset = base + count, offset + count - 1
        keep = (lane_slot == slot_of) & (lane_row < ranks[0, b])
        spread[b * rank:(b + 1) * rank, :] = jnp.where(keep, wide[b * rank:(b + 1) * rank, :], 0.0).astype(BF16)

    relay(last, 0, True)

    landed(ext_near.at[0:quarter], near_recv.at[0])
    own_mate = whole(0, 3 - core)
    landed(own_mate, mate_recv.at[0])
    lanes = comps * width
    x = jnp.dot(own_pick[:, :2 * tile], raw[0, 2:4].reshape(2 * tile, lanes), preferred_element_type=F32)
    x = x + jnp.dot(own_pick[:, 2 * tile:], ext_near[...], preferred_element_type=F32)
    x = x.astype(BF16)
    piece = jnp.zeros((2 * piece_rows, width), F32)
    for d in range(comps):
        weights = jnp.concatenate(
            [bases[level, d, h * cut:(h + 1) * cut] for h in range(2) for level in range(levels)], axis=0
        )
        piece = piece + jnp.dot(weights, x[:, d * width:(d + 1) * width], preferred_element_type=F32)
    for h in range(2):
        piece_out[h] = piece[h * piece_rows:(h + 1) * piece_rows]
    push(piece_out.at[1 - core], piece_mate, pair_recv.at[0], mate)
    for by in (-2, 2):
        order_landed(by)
    orders[2] = order[...]
    landed(piece_mate, pair_recv.at[0])
    pair = piece_out[core] + piece_mate[...]
    piece_out[2] = pair
    pieces[c // 2] = pair

    def piece_copy(d):
        return pltpu.make_async_remote_copy(
            src_ref=piece_out.at[2], dst_ref=pieces.at[c // 2], send_sem=piece_send.at[d],
            recv_sem=piece_recv.at[c // 2], device_id=at_clu(2 * d), device_id_type=MESH,
        )

    def start_piece(d, carry):
        piece_copy(d).start()
        return carry

    lax.fori_loop(1, half, start_piece, 0)
    send_z(last, 2)
    send_ext(0, 0)
    for d in range(comps):
        send_z(0, d)

    first = c - core - 2
    for j in range(near_count):
        spot = near_col[0, j] - c + 2
        spot = jnp.where(spot < 0, spot + n, spot)
        spot = jnp.where(spot >= n, spot - n, spot)
        one_hot(orders[jnp.clip(spot, 0, 4)], first, slots, picks.at[j * tile:(j + 1) * tile])
    relay(last, 1, True)

    def await_piece(d, carry):
        source = lax.rem(c // 2 + d, half)
        landed(pieces.at[source], piece_recv.at[source])
        return carry

    lax.fori_loop(1, half, await_piece, 0)
    at = 0
    for level, count in blocks:
        members = half // count
        own = (c // 2) // members
        for step in range(count - 1):
            k = lax.rem(own + 1 + step, count)
            entry = lax.fori_loop(
                0, members,
                lambda m, acc, k=k, members=members, level=level: acc
                + pieces[k * members + m, level * cut:(level + 1) * cut, :],
                jnp.zeros((cut, width), F32),
            )
            table_out[at:at + cut, :] = entry
            at += cut
    tables[0, core] = table_out[...]
    for i in range(1, groups):
        push(table_out, tables.at[i, core], table_recv.at[i, core], at_grp(i))
    push(table_out, tables.at[0, core], table_recv.at[0, core], mate)

    relay(last, 2, True)
    small[7].wait()
    small[8].wait()

    def gathered(i):
        x = jnp.dot(picks[:, :slots * tile], raw[i].reshape(slots * tile, lanes), preferred_element_type=F32)
        x = x + jnp.dot(picks[:, slots * tile:], ext[i], preferred_element_type=F32)
        return x.astype(BF16)

    def near(i):
        x = gathered(i)
        acc = jnp.zeros((rows, width), F32)
        for j in range(near_count):
            mine = jnp.concatenate(
                [x[j * tile:(j + 1) * tile, d * width:(d + 1) * width] for d in range(comps)], axis=0
            )
            acc = acc + jnp.dot(tiles[j], mine, preferred_element_type=F32)
        return acc

    landed(ext_in(last), ext_recv.at[last])
    for to, at in ((1, 2), (2, 1)):
        push(ext_in(last), ext_in(at), ext_recv.at[at], at_grp(to))
    for i in (1, 2, last):
        own_arrived(i) if i != last else None
        landed(whole(i, 3 - core), mate_recv.at[i])

    for i in (1, 2):
        relay(i, 0)
    for i in range(1, groups):
        landed(tables.at[i, core], table_recv.at[i, core])
        push(tables.at[i, core], tables.at[i, core], table_recv.at[i, core], mate)
    for d in range(comps):
        take(last, d)
    total[last] = near(last)
    for i in (1, 2):
        relay(i, 1)

    for i in range(groups):
        landed(tables.at[i, 1 - core], table_recv.at[i, 1 - core])
    table = jnp.concatenate([tables[i].reshape(2 * table_rows, width) for i in range(groups)], axis=1)
    high = table.astype(BF16)
    low = (table - high.astype(F32)).astype(BF16)
    mixed = jnp.dot(spread[...], high, preferred_element_type=F32)
    mixed = mixed + jnp.dot(spread[...], low, preferred_element_type=F32)
    for b in range(far_count):
        coupled[b * rank:(b + 1) * rank, :] = (mixed[b * rank:(b + 1) * rank, :] * scale[0, b]).astype(BF16)
    far = lax.dot_general(basis[...], coupled[...], (((0,), (0,)), ((), ())), preferred_element_type=F32)

    def send_y(i, value):
        y_out[i] = value.astype(BF16)
        push(y_out.at[i], y_in.at[i], y_recv.at[i], at_grp(i))

    send_y(last, total[last] + far[:, last * width:])
    for i in range(last):
        total[i] = far[:, i * width:(i + 1) * width]
    for i in (1, 2):
        relay(i, 2)
    for i in (1, 2):
        for d in range(comps):
            take(i, d)
        landed(ext_in(i), ext_recv.at[i])
        send_y(i, total[i] + near(i))
    for d in range(comps):
        relay(0, d)
    landed(ext_in(0), ext_recv.at[0])
    for d in range(comps):
        take(0, d)
    answer = total[0] + near(0)
    for i in range(1, groups):
        landed(y_in.at[i], y_recv.at[i])
        answer = answer + y_in[i].astype(F32)
    out[...] = answer.reshape(comps, tile, width)

    for copy in sends:
        copy.wait_send()

    def end_piece(d, carry):
        piece_copy(d).wait_send()
        return carry

    lax.fori_loop(1, half, end_piece, 0)


def solution(mesh):
    n, groups = mesh.shape["clu"], mesh.shape["grp"]

    def on_device(forces, order, bases, near_tiles, near_col, far_basis, far_coupling, far_scale, far_rank, far_target):
        comps, tile, columns = forces.shape
        levels, rank = bases.shape[:2]
        near_count, far_count = near_tiles.shape[1], far_basis.shape[1]
        width, rows, quarter = columns // groups, comps * tile, tile // 4
        lanes = comps * width
        cut = rank // 2
        piece_rows = levels * cut
        table_rows = sum(2 ** (level + 1) - 1 for level in range(levels)) * cut
        slots = 6
        pad = 128
        vmem, hbm = (pl.BlockSpec(memory_space=m) for m in (pltpu.VMEM, pl.ANY))
        dma = pltpu.SemaphoreType.DMA
        operands = (
            forces,
            order.reshape(1, tile),
            jnp.transpose(bases, (0, 2, 1, 3)),
            near_tiles.reshape(near_count, rows, rows),
            near_col,
            far_basis.reshape(far_count * rank, rows),
            far_coupling.reshape(far_count * rank, rank),
            far_scale,
            far_rank,
            far_target,
        )
        return pl.pallas_call(
            functools.partial(kernel, n, groups, levels, rank),
            out_shape=jax.ShapeDtypeStruct((comps, tile, width), F32),
            in_specs=[hbm] * len(operands),
            out_specs=vmem,
            scratch_shapes=[
                pltpu.VMEM((1, tile), jnp.int32),
                pltpu.VMEM((levels, comps, rank, tile), BF16),
                pltpu.VMEM((far_count * rank, rank), BF16),
                pltpu.SMEM((1, near_count), jnp.int32),
                pltpu.SMEM((1, far_count), F32),
                pltpu.SMEM((1, far_count), jnp.int32),
                pltpu.SMEM((1, far_count), jnp.int32),
                pltpu.VMEM((groups, slots, tile, lanes), BF16),
                pltpu.VMEM((groups, pad, lanes), BF16),
                pltpu.VMEM((2, quarter, lanes), BF16),
                pltpu.VMEM((pad, lanes), BF16),
                pltpu.VMEM((5, 1, tile), jnp.int32),
                pltpu.VMEM((near_count, rows, rows), BF16),
                pltpu.VMEM((far_count * rank, rows), BF16),
                pltpu.VMEM((far_count * rank, 2 * table_rows), BF16),
                pltpu.VMEM((near_count * tile, slots * tile + pad), BF16),
                pltpu.VMEM((tile, 2 * tile + pad), BF16),
                pltpu.VMEM((3, piece_rows, width), F32),
                pltpu.VMEM((piece_rows, width), F32),
                pltpu.VMEM((n // 2, piece_rows, width), F32),
                pltpu.VMEM((table_rows, width), F32),
                pltpu.VMEM((groups, 2, table_rows, width), F32),
                pltpu.VMEM((far_count * rank, columns), BF16),
                pltpu.VMEM((groups, rows, width), F32),
                pltpu.VMEM((groups, rows, width), BF16),
                pltpu.VMEM((groups, rows, width), BF16),
                dma((9,)), dma((groups,)), dma((SENDS,)), dma((n // 2,)),
                dma((5,)), dma((groups,)), dma((groups, slots, comps)), dma((groups,)), dma((1,)),
                dma((1,)), dma((n // 2,)), dma((groups, 2)), dma((groups,)),
            ],
            compiler_params=pltpu.CompilerParams(
                collective_id=0, has_side_effects=True, vmem_limit_bytes=28 * 1024 * 1024
            ),
        )(*(pltpu.with_memory_space_constraint(operand, pltpu.HBM) for operand in operands))

    placed = (
        P(None, "clu", None),
        P("clu"),
        P(None, None, None, "clu"),
        P("clu", "grp", None, None),
        P("clu", "grp"),
        P("clu", "grp", None, None),
        P("clu", "grp", None, None),
        P("clu", "grp"),
        P("clu", "grp"),
        P("clu", "grp"),
    )
    return jax.shard_map(
        on_device, mesh=mesh, in_specs=placed, out_specs=P(None, "clu", "grp"), check_vma=False
    )
```

time: 51.8 us -> 41.1 us (0.79)
  Pallas kernels: 49.9 us -> 40.2 us
  local copies, waits for them, and re-layouts: 1.77 us -> 0.75 us
    pallas_call x1, Pallas kernels: 49.9 us -> 40.2 us  [on_device(): pl.pallas_call(functools.partial(kernel, n, groups, levels, rank), out_sh...]
    unnamed x1, local copies, waits for them, and re-layouts: 1.77 us -> 0.75 us
where the time goes in v1:
time: 41.1 us; the launch traced here: 41 us
  Pallas kernels  40.2 us (98%)
  local copies, waits for them, and re-layouts  0.75 us (2%)
    pallas_call x1, Pallas kernels, on_device(): pl.pallas_call(functools.partial(kernel, n, groups, levels, rank), out_sh...  40.2 us

profile of v1, /device:TPU:0, one launch (start us, length us, event | category | flops | bytes accessed | tf_op | source)
XLA Modules:
  0.0 41.0 jit_solution(553562894570814529)
XLA Ops:
  0.0 40.2 %shard_map.100 = f32[3,256,128]{2,1,0:T(8,128)S(1)} custom-call(bf16[3,256,512]{2,1,0:T(8,128)(2,1)} %forces.1, s32[1,256]{1,0:T(1,128)} %bitcast.9, bf16[2,3,32,256]{3,2,1,0:T(8,128)(2,1)} %bitcast.8, bf16[2,768,768]{2,1,0:T(8,128)(2,1)} %bitcast.5, s32[1,2]{1,0:T(1,128)} %near_col_hbm.1, bf16[512,768]{1,0:T(8,128)(2,1)} %bitcast.6, ...), custom_call_target="tpu_custom_call" | custom-call | tf_op jit(solution)/shard_map/pallas_call | solution.py:388
  40.2 0.7 %copy.12 = f32[3,256,128]{2,1,0:T(8,128)} copy(f32[3,256,128]{2,1,0:T(8,128)S(1)} %shard_map.100) | data formatting | bytes 786432

commit v2 on v1

v2 whole, which is shorter than its diff:
```python
import functools

import jax
import jax.numpy as jnp
from jax import lax
from jax.experimental import pallas as pl
from jax.experimental.pallas import tpu as pltpu
from jax.sharding import PartitionSpec as P

MESH = pl.DeviceIdType.MESH
F32, BF16 = jnp.float32, jnp.bfloat16
SENDS = 48


def kernel(
    n, groups, levels, rank, comps,
    forces, order_hbm, bases_hbm, tiles_hbm, near_col_hbm, basis_hbm, coupling_hbm, scale_hbm, ranks_hbm, targets_hbm,
    out,
    order, bases, coupling, near_col, scale, ranks, targets, tiles, basis,
    ext_out, ext_near, orders, spread, picks, own_pick, piece_out, piece_mate, pieces,
    table, w_out, w_in, w_own, w_all, y_out, y_in, totals, pair_total,
    local_sem, own_sem, send_sem, piece_send, order_recv, mate_recv, z_recv, across_recv, ext_recv, near_recv,
    pair_recv, piece_recv, table_recv, w_recv, y_recv,
    *blocks,
):
    g, c = lax.axis_index("grp"), lax.axis_index("clu")
    core = lax.rem(c, 2)
    tile, columns = forces.shape[1:]
    width = columns // groups
    quarter = tile // 4
    rows = comps * tile
    near_count = tiles.shape[0]
    far_count = targets.shape[1]
    half = n // 2
    cut = rank // 2
    piece_rows = levels * cut
    spans = [(level, 2 ** (level + 1)) for level in range(levels)]
    table_rows = sum(count - 1 for _, count in spans) * cut
    last = groups - 1
    own_blocks, far_blocks, side_blocks = (blocks[at * comps:(at + 1) * comps] for at in range(3))
    edge = 7 * core

    def at_clu(by):
        return {"grp": g, "clu": lax.rem(c + by + n, n)}

    partners = (g, g + 1 - 2 * lax.rem(g, 2), lax.rem(g + 2, groups), groups - 1 - g)

    def at_grp(i):
        return {"grp": partners[i], "clu": c}

    mate = {"grp": g, "clu": c + 1 - 2 * core}
    sends = []

    def remote(src, dst, recv, where, index=0):
        return pltpu.make_async_remote_copy(
            src_ref=src, dst_ref=dst, send_sem=send_sem.at[index], recv_sem=recv, device_id=where, device_id_type=MESH
        )

    def push(copies, bytes_of):
        assert len(sends) < SENDS
        for src, dst, recv, where in copies:
            remote(src, dst, recv, where, len(sends)).start()
        sends.append(remote(bytes_of, bytes_of, near_recv.at[0], mate, len(sends)))

    def landed(ref, recv):
        remote(ref, ref, recv, mate).wait_recv()

    def several(count):
        return own_blocks[0].at[0:count]

    def columns_of(i, d):
        return forces.at[d, :, pl.ds(pl.multiple_of(partners[i] * width, width), width)]

    def part(i, p, d):
        if i == 0:
            return own_blocks[d].at[p]
        if i == last:
            return far_blocks[d].at[p]
        return side_blocks[d].at[p, :, pl.ds((i - 1) * width, width)]

    def edge_rows(i, p, d):
        if i == 0:
            return own_blocks[d].at[p, 0:quarter]
        if i == last:
            return far_blocks[d].at[p, 0:quarter]
        return side_blocks[d].at[p, 0:quarter, pl.ds((i - 1) * width, width)]

    small = [
        pltpu.make_async_copy(src, dst, local_sem.at[at])
        for at, (src, dst) in enumerate((
            (order_hbm, order), (coupling_hbm, coupling), (targets_hbm, targets), (ranks_hbm, ranks),
            (scale_hbm, scale), (basis_hbm, basis), (bases_hbm, bases), (near_col_hbm, near_col), (tiles_hbm, tiles),
        ))
    ]
    for copy in small[:6]:
        copy.start()
    for i in (last, 0, 1, 2):
        for d in range(comps):
            pltpu.make_async_copy(columns_of(i, d), part(i, 3 + core, d), own_sem.at[i]).start()
    for copy in small[6:]:
        copy.start()

    barrier = pltpu.get_barrier_semaphore()

    def greet(d, carry):
        pl.semaphore_signal(barrier, inc=1, device_id=at_clu(d), device_id_type=MESH)
        return carry

    lax.fori_loop(1, n, greet, 0)
    for d in range(1, groups):
        pl.semaphore_signal(barrier, inc=1, device_id=at_grp(d), device_id_type=MESH)

    for block in blocks:
        block[edge, quarter:, :] = jnp.zeros((tile - quarter, block.shape[2]), BF16)
    ext_near[:, quarter:, :] = jnp.zeros((comps, ext_near.shape[1] - quarter, width), BF16)

    for copy in small[1:5]:
        copy.wait()
    lane = lax.broadcasted_iota(jnp.int32, (rank, 2 * table_rows), 1)
    row = lax.broadcasted_iota(jnp.int32, (rank, 2 * table_rows), 0)
    lane_row = (lane // table_rows) * cut + lax.rem(lane, cut)
    lane_slot = lax.rem(lane, table_rows) // cut
    repeat = (lane_row == row).astype(F32).astype(BF16)
    wide = jnp.dot(coupling[...], repeat, preferred_element_type=F32)
    for b in range(far_count):
        target = targets[0, b]
        slot_of, base, offset = target, 0, 0
        for level, count in spans:
            own = (c // 2) // (half // count)
            here = target - base - own - 1
            here = jnp.where(here < 0, here + count, here) + offset
            slot_of = jnp.where((target >= base) & (target < base + count), here, slot_of)
            base, offset = base + count, offset + count - 1
        keep = (lane_slot == slot_of) & (lane_row < ranks[0, b])
        scaled = jnp.where(keep, wide[b * rank:(b + 1) * rank, :] * scale[0, b], 0.0)
        high = scaled.astype(BF16)
        spread[b * rank:(b + 1) * rank, :2 * table_rows] = high
        spread[b * rank:(b + 1) * rank, 2 * table_rows:] = (scaled - high.astype(F32)).astype(BF16)
    small[5].wait()
    folded = lax.dot_general(basis[...], spread[...], (((0,), (0,)), ((), ())), preferred_element_type=F32)
    folded = folded[:, :2 * table_rows] + folded[:, 2 * table_rows:]
    w_out[...] = folded.reshape(groups, rows // groups, 2 * table_rows)

    sub = lax.broadcasted_iota(jnp.int32, (tile, tile), 0)
    lan = lax.broadcasted_iota(jnp.int32, (tile, tile), 1)
    upto = (sub <= lan).astype(BF16)

    def ranked(chosen):
        spots = jnp.broadcast_to(chosen.astype(F32), (8, tile)).astype(BF16)
        return (jnp.dot(spots, upto, preferred_element_type=F32)[0:1, :] - 1.0).astype(jnp.int32)

    def wrapped(spot):
        spot = jnp.where(spot < 0, spot + n * tile, spot)
        return jnp.where(spot >= n * tile, spot - n * tile, spot)

    def one_hot(spot, store, count):
        down = jnp.broadcast_to(spot.astype(F32), (128, tile)).T
        at = lax.broadcasted_iota(jnp.int32, (tile, 128), 1).astype(F32)
        for j in range(count):
            store(j, (down == at + float(j * 128)).astype(F32).astype(BF16))

    small[0].wait()
    spot = wrapped(order[...] - (c - core) * tile)
    beyond = spot >= 2 * tile
    spot = jnp.where(beyond, 2 * tile + ranked(beyond), spot)

    def store_own(j, value):
        own_pick[:, j * 128:(j + 1) * 128] = value

    one_hot(spot, store_own, own_pick.shape[1] // 128)

    def own_arrived(i):
        pltpu.make_async_copy(several(comps), several(comps), own_sem.at[i]).wait()

    own_arrived(last)
    pl.semaphore_wait(barrier, n - 1 + groups - 1)

    for by in (-1, 1, -2, 2):
        push([(order, orders.at[2 - by], order_recv.at[2 - by], at_clu(by))], order)

    def z_copies(i, d):
        return [
            (part(i, 3 + core, d), part(i, 1 + core, d), z_recv.at[i, d, 0], at_clu(2)),
            (part(i, 3 + core, d), part(i, 5 + core, d), z_recv.at[i, d, 1], at_clu(-2)),
        ]

    push(z_copies(last, 0), several(2))
    push(
        [(w_out.at[partners[i]], w_in.at[i], w_recv.at[0, i], at_grp(i)) for i in range(1, groups)],
        w_out.at[0:groups - 1],
    )

    def send_mate(i):
        push([(part(i, 3 + core, d), part(i, 3 + core, d), mate_recv.at[i], mate) for d in range(comps)], several(comps))

    send_mate(last)
    own_arrived(0)
    send_mate(0)

    def order_landed(by):
        landed(orders.at[2 + by], order_recv.at[2 + by])

    for by in (-1, 1):
        order_landed(by)
    away = orders[1 + 2 * core] - c * tile
    chosen = (away >= 0) & (away < tile)
    place = jnp.where(chosen, ranked(chosen), -1)
    left = (lax.broadcasted_iota(jnp.int32, (128, tile), 0) == place).astype(F32).astype(BF16)
    right = (sub == away).astype(F32).astype(BF16)
    pick = lax.dot_general(left, right, (((1,), (1,)), ((), ())), preferred_element_type=F32).astype(BF16)

    def pick_edge(at, own):
        for d in range(comps):
            ext_out[at, d] = jnp.dot(pick, own[d][3 + core], preferred_element_type=F32).astype(BF16)[:quarter]

    pick_edge(1, far_blocks)
    push(
        [
            (ext_out.at[1, d], edge_rows(last, 7 - edge, d), ext_recv.at[last], at_clu(6 * core - 3))
            for d in range(comps)
        ],
        ext_out.at[1],
    )
    for d in range(1, comps):
        push(z_copies(last, d), several(2))
    pick_edge(0, own_blocks)
    push([(ext_out.at[0], ext_near.at[:, 0:quarter], near_recv.at[0], at_clu(2 * core - 1))], ext_out.at[0])
    push(z_copies(0, 0), several(2))
    for i in (1, 2):
        own_arrived(i)
        send_mate(i)

    for by in (-2, 2):
        order_landed(by)
    orders[2] = order[...]
    small[7].wait()
    starts = []
    for j in range(near_count):
        spot0 = near_col[0, j] - c + 2
        spot0 = jnp.where(spot0 < 0, spot0 + n, spot0)
        spot0 = jnp.clip(jnp.where(spot0 >= n, spot0 - n, spot0), 0, 4)
        starts.append(spot0 + core)
        spot = wrapped(orders[spot0] - (c + spot0 - 3) * tile)
        low = 2 * core * tile
        beyond = (spot >= low) & (spot < low + tile) & (spot0 == 4 * core)
        spot = jnp.where(beyond, low + ranked(beyond), spot)

        def store_pick(at, value, j=j):
            picks[j, :, at * 128:(at + 1) * 128] = value

        one_hot(spot, store_pick, picks.shape[2] // 128)

    def relay(i, d):
        copies = []
        for side, p in enumerate((1 + core, 5 + core)):
            landed(part(i, p, d), z_recv.at[i, d, side])
            copies.append((part(i, p, d), part(i, p, d), across_recv.at[i, d], mate))
            if i == last:
                for to, at in ((1, 2), (2, 1)):
                    copies.append((part(i, p, d), part(at, p, d), z_recv.at[at, d, side], at_grp(to)))
        push(copies, several(len(copies)))

    def take(i, d):
        landed(several(2), across_recv.at[i, d])

    relay(last, 0)

    for i in range(1, groups):
        landed(w_in.at[i], w_recv.at[0, i])
    summed = w_out[g]
    for i in range(1, groups):
        summed = summed + w_in[i]
    w_own[...] = summed.astype(BF16)
    w_all[g] = summed.astype(BF16)
    push([(w_own, w_all.at[g], w_recv.at[1, i], at_grp(i)) for i in range(1, groups)], w_all.at[0:groups - 1])

    small[6].wait()
    landed(ext_out.at[0], near_recv.at[0])
    push(
        [
            (ext_near.at[d, 0:quarter], edge_rows(0, edge, d), ext_recv.at[0], at_clu(2 - 4 * core))
            for d in range(comps)
        ],
        ext_out.at[0],
    )
    landed(several(comps), mate_recv.at[0])
    piece = jnp.zeros((2 * piece_rows, width), F32)
    for d in range(comps):
        x = jnp.dot(own_pick[:, :2 * tile], own_blocks[d][3:5].reshape(2 * tile, width), preferred_element_type=F32)
        x = x + jnp.dot(own_pick[:, 2 * tile:], ext_near[d], preferred_element_type=F32)
        weights = jnp.concatenate(
            [bases[level, d, h * cut:(h + 1) * cut] for h in range(2) for level in range(levels)], axis=0
        )
        piece = piece + jnp.dot(weights, x.astype(BF16), preferred_element_type=F32)
    for h in range(2):
        piece_out[h] = piece[h * piece_rows:(h + 1) * piece_rows]
    push([(piece_out.at[1 - core], piece_mate, pair_recv.at[0], mate)], piece_mate)
    relay(last, 1)
    landed(piece_mate, pair_recv.at[0])
    pair = piece_out[core] + piece_mate[...]
    piece_out[2] = pair
    pieces[c // 2] = pair

    def piece_copy(d):
        return pltpu.make_async_remote_copy(
            src_ref=piece_out.at[2], dst_ref=pieces.at[c // 2], send_sem=piece_send.at[d],
            recv_sem=piece_recv.at[c // 2], device_id=at_clu(2 * d), device_id_type=MESH,
        )

    def start_piece(d, carry):
        piece_copy(d).start()
        return carry

    lax.fori_loop(1, half, start_piece, 0)
    for d in range(1, comps):
        push(z_copies(0, d), several(2))

    landed(ext_out.at[1], ext_recv.at[last])
    push(
        [
            (edge_rows(last, edge, d), edge_rows(at, edge, d), ext_recv.at[at], at_grp(to))
            for to, at in ((1, 2), (2, 1)) for d in range(comps)
        ],
        ext_out,
    )
    landed(several(comps), mate_recv.at[last])
    small[8].wait()

    def near(block, d):
        acc = None
        for j in range(near_count):
            held = block[d][pl.ds(starts[j], 3)].reshape(3 * tile, block[d].shape[2])
            x = jnp.dot(picks[j], held, preferred_element_type=F32).astype(BF16)
            term = jnp.dot(tiles[j, :, d * tile:(d + 1) * tile], x, preferred_element_type=F32)
            acc = term if acc is None else acc + term
        return acc

    take(last, 0)
    totals[...] = near(far_blocks, 0)
    relay(last, 2)
    for i in (1, 2):
        relay(i, 0)
    take(last, 1)
    totals[...] += near(far_blocks, 1)
    for i in (1, 2):
        relay(i, 1)

    def await_piece(d, carry):
        source = lax.rem(c // 2 + d, half)
        landed(pieces.at[source], piece_recv.at[source])
        return carry

    lax.fori_loop(1, half, await_piece, 0)
    at = 0
    for level, count in spans:
        members = half // count
        own = (c // 2) // members
        for step in range(count - 1):
            k = lax.rem(own + 1 + step, count)
            entry = lax.fori_loop(
                0, members,
                lambda m, acc, k=k, members=members, level=level: acc
                + pieces[k * members + m, level * cut:(level + 1) * cut, :],
                jnp.zeros((cut, width), F32),
            )
            table[core, at:at + cut, :] = entry
            at += cut
    push([(table.at[core], table.at[core], table_recv.at[0], mate)], table.at[0])

    def send_y(i, value):
        y_out[i] = value.astype(BF16)
        push([(y_out.at[i], y_in.at[i], y_recv.at[i], at_grp(i))], y_out.at[i])

    take(last, 2)
    send_y(last, totals[...] + near(far_blocks, 2))

    for i in (1, 2):
        landed(several(comps), mate_recv.at[i])
        landed(ext_out.at[0], ext_recv.at[i])
        take(i, 0)
    pair_total[...] = near(side_blocks, 0)
    for i in (1, 2):
        relay(i, 2)
    relay(0, 0)
    for i in (1, 2):
        take(i, 1)
    pair_total[...] += near(side_blocks, 1)
    for i in (1, 2):
        take(i, 2)
    both = pair_total[...] + near(side_blocks, 2)
    for i in (1, 2):
        send_y(i, both[:, (i - 1) * width:i * width])

    for i in range(1, groups):
        landed(w_own, w_recv.at[1, i])
    landed(table.at[0], table_recv.at[0])
    entries = table[...].reshape(2 * table_rows, width)
    high = entries.astype(BF16)
    low = (entries - high.astype(F32)).astype(BF16)
    weights = w_all[...].reshape(rows, 2 * table_rows)
    answer = jnp.dot(weights, high, preferred_element_type=F32) + jnp.dot(weights, low, preferred_element_type=F32)
    landed(ext_out.at[0], ext_recv.at[0])
    relay(0, 1)
    take(0, 0)
    totals[...] = answer + near(own_blocks, 0)
    relay(0, 2)
    take(0, 1)
    totals[...] += near(own_blocks, 1)
    for i in range(1, groups):
        landed(y_in.at[i], y_recv.at[i])
        totals[...] += y_in[i].astype(F32)
    for copy in sends:
        copy.wait_send()

    def end_piece(d, carry):
        piece_copy(d).wait_send()
        return carry

    lax.fori_loop(1, half, end_piece, 0)
    take(0, 2)
    out[...] = (totals[...] + near(own_blocks, 2)).reshape(comps, tile, width)


def solution(mesh):
    n, groups = mesh.shape["clu"], mesh.shape["grp"]

    def on_device(forces, order, bases, near_tiles, near_col, far_basis, far_coupling, far_scale, far_rank, far_target):
        comps, tile, columns = forces.shape
        levels, rank = bases.shape[:2]
        near_count, far_count = near_tiles.shape[1], far_basis.shape[1]
        width, rows, quarter = columns // groups, comps * tile, tile // 4
        cut = rank // 2
        piece_rows = levels * cut
        table_rows = sum(2 ** (level + 1) - 1 for level in range(levels)) * cut
        slots = 8
        pad = 128
        vmem, hbm = (pl.BlockSpec(memory_space=m) for m in (pltpu.VMEM, pl.ANY))
        dma = pltpu.SemaphoreType.DMA
        operands = (
            forces,
            order.reshape(1, tile),
            jnp.transpose(bases, (0, 2, 1, 3)),
            near_tiles.reshape(near_count, rows, rows),
            near_col,
            far_basis.reshape(far_count * rank, rows),
            far_coupling.reshape(far_count * rank, rank),
            far_scale,
            far_rank,
            far_target,
        )
        return pl.pallas_call(
            functools.partial(kernel, n, groups, levels, rank, comps),
            out_shape=jax.ShapeDtypeStruct((comps, tile, width), F32),
            in_specs=[hbm] * len(operands),
            out_specs=vmem,
            scratch_shapes=[
                pltpu.VMEM((1, tile), jnp.int32),
                pltpu.VMEM((levels, comps, rank, tile), BF16),
                pltpu.VMEM((far_count * rank, rank), BF16),
                pltpu.SMEM((1, near_count), jnp.int32),
                pltpu.SMEM((1, far_count), F32),
                pltpu.SMEM((1, far_count), jnp.int32),
                pltpu.SMEM((1, far_count), jnp.int32),
                pltpu.VMEM((near_count, rows, rows), BF16),
                pltpu.VMEM((far_count * rank, rows), BF16),
                pltpu.VMEM((2, comps, quarter, width), BF16),
                pltpu.VMEM((comps, pad, width), BF16),
                pltpu.VMEM((5, 1, tile), jnp.int32),
                pltpu.VMEM((far_count * rank, 4 * table_rows), BF16),
                pltpu.VMEM((near_count, tile, 3 * tile), BF16),
                pltpu.VMEM((tile, 2 * tile + pad), BF16),
                pltpu.VMEM((3, piece_rows, width), F32),
                pltpu.VMEM((piece_rows, width), F32),
                pltpu.VMEM((n // 2, piece_rows, width), F32),
                pltpu.VMEM((2, table_rows, width), F32),
                pltpu.VMEM((groups, rows // groups, 2 * table_rows), F32),
                pltpu.VMEM((groups, rows // groups, 2 * table_rows), F32),
                pltpu.VMEM((rows // groups, 2 * table_rows), BF16),
                pltpu.VMEM((groups, rows // groups, 2 * table_rows), BF16),
                pltpu.VMEM((groups, rows, width), BF16),
                pltpu.VMEM((groups, rows, width), BF16),
                pltpu.VMEM((rows, width), F32),
                pltpu.VMEM((rows, 2 * width), F32),
                dma((9,)), dma((groups,)), dma((SENDS,)), dma((n // 2,)),
                dma((5,)), dma((groups,)), dma((groups, comps, 2)), dma((groups, comps)), dma((groups,)), dma((1,)),
                dma((1,)), dma((n // 2,)), dma((1,)), dma((2, groups)), dma((groups,)),
                *(pltpu.VMEM((slots, tile, size), BF16) for size in (width, width, 2 * width) for _ in range(comps)),
            ],
            compiler_params=pltpu.CompilerParams(
                collective_id=0, has_side_effects=True, vmem_limit_bytes=28 * 1024 * 1024
            ),
        )(*(pltpu.with_memory_space_constraint(operand, pltpu.HBM) for operand in operands))

    placed = (
        P(None, "clu", None),
        P("clu"),
        P(None, None, None, "clu"),
        P("clu", "grp", None, None),
        P("clu", "grp"),
        P("clu", "grp", None, None),
        P("clu", "grp", None, None),
        P("clu", "grp"),
        P("clu", "grp"),
        P("clu", "grp"),
    )
    return jax.shard_map(
        on_device, mesh=mesh, in_specs=placed, out_specs=P(None, "clu", "grp"), check_vma=False
    )
```

time: 41.1 us -> 42.3 us (1.029)
  Pallas kernels: 40.2 us -> 41.4 us
    pallas_call x1, Pallas kernels: 40.2 us -> 41.4 us  [on_device(): pl.pallas_call(functools.partial(kernel, n, groups, levels, rank, comps),...]
where the time goes in v2:
time: 42.3 us; the launch traced here: 42.2 us
  Pallas kernels  41.4 us (98%)
  local copies, waits for them, and re-layouts  0.75 us (2%)
    pallas_call x1, Pallas kernels, on_device(): pl.pallas_call(functools.partial(kernel, n, groups, levels, rank, comps),...  41.4 us

profile of v2, /device:TPU:0, one launch (start us, length us, event | category | flops | bytes accessed | tf_op | source)
XLA Modules:
  0.0 42.2 jit_solution(13403165861257945104)
XLA Ops:
  0.0 41.4 %shard_map.100 = f32[3,256,128]{2,1,0:T(8,128)S(1)} custom-call(bf16[3,256,512]{2,1,0:T(8,128)(2,1)} %forces.1, s32[1,256]{1,0:T(1,128)} %bitcast.9, bf16[2,3,32,256]{3,2,1,0:T(8,128)(2,1)} %bitcast.8, bf16[2,768,768]{2,1,0:T(8,128)(2,1)} %bitcast.5, s32[1,2]{1,0:T(1,128)} %near_col_hbm.1, bf16[512,768]{1,0:T(8,128)(2,1)} %bitcast.6, ...), custom_call_target="tpu_custom_call" | custom-call | tf_op jit(solution)/shard_map/pallas_call | solution.py:451
  41.4 0.7 %copy.12 = f32[3,256,128]{2,1,0:T(8,128)} copy(f32[3,256,128]{2,1,0:T(8,128)S(1)} %shard_map.100) | data formatting | bytes 786432

commit v3 on v2

--- a/solution.py
+++ b/solution.py
@@ -18,9 +18,9 @@
     out,
     order, bases, coupling, near_col, scale, ranks, targets, tiles, basis,
     ext_out, ext_near, orders, spread, picks, own_pick, piece_out, piece_mate, pieces,
-    table, w_out, w_in, w_own, w_all, y_out, y_in, totals, pair_total,
+    table, w_out, w_in, w_own, w_all, y_out, y_in, y_mid, totals, pair_total,
     local_sem, own_sem, send_sem, piece_send, order_recv, mate_recv, z_recv, across_recv, ext_recv, near_recv,
-    pair_recv, piece_recv, table_recv, w_recv, y_recv,
+    pair_recv, piece_recv, table_recv, w_recv, y_recv, mid_recv,
     *blocks,
 ):
     g, c = lax.axis_index("grp"), lax.axis_index("clu")
@@ -184,7 +184,8 @@
             (part(i, 3 + core, d), part(i, 5 + core, d), z_recv.at[i, d, 1], at_clu(-2)),
         ]
 
-    push(z_copies(last, 0), several(2))
+    for d in range(comps - 1):
+        push(z_copies(last, d), several(2))
     push(
         [(w_out.at[partners[i]], w_in.at[i], w_recv.at[0, i], at_grp(i)) for i in range(1, groups)],
         w_out.at[0:groups - 1],
@@ -221,11 +222,11 @@
         ],
         ext_out.at[1],
     )
-    for d in range(1, comps):
-        push(z_copies(last, d), several(2))
+    push(z_copies(last, comps - 1), several(2))
     pick_edge(0, own_blocks)
     push([(ext_out.at[0], ext_near.at[:, 0:quarter], near_recv.at[0], at_clu(2 * core - 1))], ext_out.at[0])
-    push(z_copies(0, 0), several(2))
+    for d in range(comps - 1):
+        push(z_copies(0, d), several(2))
     for i in (1, 2):
         own_arrived(i)
         send_mate(i)
@@ -263,7 +264,31 @@
     def take(i, d):
         landed(several(2), across_recv.at[i, d])
 
+    def near(block, d):
+        acc = None
+        for j in range(near_count):
+            held = block[d][pl.ds(starts[j], 3)].reshape(3 * tile, block[d].shape[2])
+            x = jnp.dot(picks[j], held, preferred_element_type=F32).astype(BF16)
+            term = jnp.dot(tiles[j, :, d * tile:(d + 1) * tile], x, preferred_element_type=F32)
+            acc = term if acc is None else acc + term
+        return acc
+
+    mid = rows // 2
+
     relay(last, 0)
+    relay(last, 1)
+    landed(ext_out.at[1], ext_recv.at[last])
+    push(
+        [
+            (edge_rows(last, edge, d), edge_rows(at, edge, d), ext_recv.at[at], at_grp(to))
+            for to, at in ((1, 2), (2, 1)) for d in range(comps)
+        ],
+        ext_out,
+    )
+    landed(several(comps), mate_recv.at[last])
+    small[8].wait()
+    take(last, 0)
+    totals[...] = near(far_blocks, 0)
 
     for i in range(1, groups):
         landed(w_in.at[i], w_recv.at[0, i])
@@ -272,17 +297,25 @@
         summed = summed + w_in[i]
     w_own[...] = summed.astype(BF16)
     w_all[g] = summed.astype(BF16)
+
+    relay(last, 2)
     push([(w_own, w_all.at[g], w_recv.at[1, i], at_grp(i)) for i in range(1, groups)], w_all.at[0:groups - 1])
+    take(last, 1)
+    totals[...] += near(far_blocks, 1)
+    for i in (1, 2):
+        relay(i, 0)
+    take(last, 2)
+    y_out[last] = (totals[...] + near(far_blocks, 2)).astype(BF16)
+    push(
+        [
+            (y_out.at[last, 0:mid], y_mid.at[0], mid_recv.at[0], at_grp(1)),
+            (y_out.at[last, mid:rows], y_mid.at[1], mid_recv.at[1], at_grp(2)),
+        ],
+        y_out.at[last],
+    )
 
     small[6].wait()
     landed(ext_out.at[0], near_recv.at[0])
-    push(
-        [
-            (ext_near.at[d, 0:quarter], edge_rows(0, edge, d), ext_recv.at[0], at_clu(2 - 4 * core))
-            for d in range(comps)
-        ],
-        ext_out.at[0],
-    )
     landed(several(comps), mate_recv.at[0])
     piece = jnp.zeros((2 * piece_rows, width), F32)
     for d in range(comps):
@@ -295,7 +328,9 @@
     for h in range(2):
         piece_out[h] = piece[h * piece_rows:(h + 1) * piece_rows]
     push([(piece_out.at[1 - core], piece_mate, pair_recv.at[0], mate)], piece_mate)
-    relay(last, 1)
+    for i in (1, 2):
+        relay(i, 1)
+
     landed(piece_mate, pair_recv.at[0])
     pair = piece_out[core] + piece_mate[...]
     piece_out[2] = pair
@@ -312,38 +347,45 @@
         return carry
 
     lax.fori_loop(1, half, start_piece, 0)
-    for d in range(1, comps):
-        push(z_copies(0, d), several(2))
-
-    landed(ext_out.at[1], ext_recv.at[last])
+    push(z_copies(0, comps - 1), several(2))
     push(
         [
-            (edge_rows(last, edge, d), edge_rows(at, edge, d), ext_recv.at[at], at_grp(to))
-            for to, at in ((1, 2), (2, 1)) for d in range(comps)
+            (ext_near.at[d, 0:quarter], edge_rows(0, edge, d), ext_recv.at[0], at_clu(2 - 4 * core))
+            for d in range(comps)
         ],
-        ext_out,
-    )
-    landed(several(comps), mate_recv.at[last])
-    small[8].wait()
-
-    def near(block, d):
-        acc = None
-        for j in range(near_count):
-            held = block[d][pl.ds(starts[j], 3)].reshape(3 * tile, block[d].shape[2])
-            x = jnp.dot(picks[j], held, preferred_element_type=F32).astype(BF16)
-            term = jnp.dot(tiles[j, :, d * tile:(d + 1) * tile], x, preferred_element_type=F32)
-            acc = term if acc is None else acc + term
-        return acc
-
-    take(last, 0)
-    totals[...] = near(far_blocks, 0)
-    relay(last, 2)
-    for i in (1, 2):
-        relay(i, 0)
-    take(last, 1)
-    totals[...] += near(far_blocks, 1)
-    for i in (1, 2):
-        relay(i, 1)
+        ext_out.at[0],
+    )
+
+    for i in (1, 2):
+        landed(several(comps), mate_recv.at[i])
+        landed(ext_out.at[0], ext_recv.at[i])
+        take(i, 0)
+    pair_total[...] = near(side_blocks, 0)
+    for i in (1, 2):
+        relay(i, 2)
+    for i in (1, 2):
+        take(i, 1)
+    pair_total[...] += near(side_blocks, 1)
+    relay(0, 0)
+    for i in (1, 2):
+        take(i, 2)
+    both = pair_total[...] + near(side_blocks, 2)
+
+    def send_y(i, h, value):
+        here = pl.ds(h * mid, mid)
+        y_out[i, h * mid:(h + 1) * mid] = value.astype(BF16)
+        push([(y_out.at[i, here], y_in.at[i, here], y_recv.at[i, h], at_grp(i))], y_mid.at[0])
+
+    def half_of(i, h):
+        return both[h * mid:(h + 1) * mid, (i - 1) * width:i * width]
+
+    send_y(1, 0, half_of(1, 0))
+    send_y(2, 1, half_of(2, 1))
+    landed(y_mid.at[1], mid_recv.at[1])
+    send_y(1, 1, half_of(1, 1) + y_mid[1].astype(F32))
+    landed(y_mid.at[0], mid_recv.at[0])
+    send_y(2, 0, half_of(2, 0) + y_mid[0].astype(F32))
+    relay(0, 1)
 
     def await_piece(d, carry):
         source = lax.rem(c // 2 + d, half)
@@ -367,30 +409,10 @@
             at += cut
     push([(table.at[core], table.at[core], table_recv.at[0], mate)], table.at[0])
 
-    def send_y(i, value):
-        y_out[i] = value.astype(BF16)
-        push([(y_out.at[i], y_in.at[i], y_recv.at[i], at_grp(i))], y_out.at[i])
-
-    take(last, 2)
-    send_y(last, totals[...] + near(far_blocks, 2))
-
-    for i in (1, 2):
-        landed(several(comps), mate_recv.at[i])
-        landed(ext_out.at[0], ext_recv.at[i])
-        take(i, 0)
-    pair_total[...] = near(side_blocks, 0)
-    for i in (1, 2):
-        relay(i, 2)
-    relay(0, 0)
-    for i in (1, 2):
-        take(i, 1)
-    pair_total[...] += near(side_blocks, 1)
-    for i in (1, 2):
-        take(i, 2)
-    both = pair_total[...] + near(side_blocks, 2)
-    for i in (1, 2):
-        send_y(i, both[:, (i - 1) * width:i * width])
-
+    landed(ext_out.at[0], ext_recv.at[0])
+    take(0, 0)
+    totals[...] = near(own_blocks, 0)
+    relay(0, 2)
     for i in range(1, groups):
         landed(w_own, w_recv.at[1, i])
     landed(table.at[0], table_recv.at[0])
@@ -399,16 +421,11 @@
     low = (entries - high.astype(F32)).astype(BF16)
     weights = w_all[...].reshape(rows, 2 * table_rows)
     answer = jnp.dot(weights, high, preferred_element_type=F32) + jnp.dot(weights, low, preferred_element_type=F32)
-    landed(ext_out.at[0], ext_recv.at[0])
-    relay(0, 1)
-    take(0, 0)
-    totals[...] = answer + near(own_blocks, 0)
-    relay(0, 2)
     take(0, 1)
-    totals[...] += near(own_blocks, 1)
-    for i in range(1, groups):
-        landed(y_in.at[i], y_recv.at[i])
-        totals[...] += y_in[i].astype(F32)
+    totals[...] += answer + near(own_blocks, 1)
+    take(0, 2)
+    totals[...] += near(own_blocks, 2)
+
     for copy in sends:
         copy.wait_send()
 
@@ -417,8 +434,10 @@
         return carry
 
     lax.fori_loop(1, half, end_piece, 0)
-    take(0, 2)
-    out[...] = (totals[...] + near(own_blocks, 2)).reshape(comps, tile, width)
+    for i in (1, 2):
+        for h in range(2):
+            landed(y_mid.at[0], y_recv.at[i, h])
+    out[...] = (totals[...] + y_in[1].astype(F32) + y_in[2].astype(F32)).reshape(comps, tile, width)
 
 
 def solution(mesh):
@@ -479,11 +498,12 @@
                 pltpu.VMEM((groups, rows // groups, 2 * table_rows), BF16),
                 pltpu.VMEM((groups, rows, width), BF16),
                 pltpu.VMEM((groups, rows, width), BF16),
+                pltpu.VMEM((2, rows // 2, width), BF16),
                 pltpu.VMEM((rows, width), F32),
                 pltpu.VMEM((rows, 2 * width), F32),
                 dma((9,)), dma((groups,)), dma((SENDS,)), dma((n // 2,)),
                 dma((5,)), dma((groups,)), dma((groups, comps, 2)), dma((groups, comps)), dma((groups,)), dma((1,)),
-                dma((1,)), dma((n // 2,)), dma((1,)), dma((2, groups)), dma((groups,)),
+                dma((1,)), dma((n // 2,)), dma((1,)), dma((2, groups)), dma((groups, 2)), dma((2,)),
                 *(pltpu.VMEM((slots, tile, size), BF16) for size in (width, width, 2 * width) for _ in range(comps)),
             ],
             compiler_params=pltpu.CompilerParams(

time: 42.3 us -> 35.6 us (0.84)
  Pallas kernels: 41.4 us -> 34.7 us
    pallas_call x1, Pallas kernels: 41.4 us -> 34.7 us  [on_device(): pl.pallas_call(functools.partial(kernel, n, groups, levels, rank, comps),...]
where the time goes in v3:
time: 35.6 us; the launch traced here: 35.5 us
  Pallas kernels  34.7 us (97%)
  local copies, waits for them, and re-layouts  0.75 us (2%)
    pallas_call x1, Pallas kernels, on_device(): pl.pallas_call(functools.partial(kernel, n, groups, levels, rank, comps),...  34.7 us
    unnamed x1, local copies, waits for them, and re-layouts  0.75 us

profile of v3, /device:TPU:0, one launch (start us, length us, event | category | flops | bytes accessed | tf_op | source)
XLA Modules:
  0.0 35.5 jit_solution(12949768510885896686)
XLA Ops:
  0.0 34.7 %shard_map.100 = f32[3,256,128]{2,1,0:T(8,128)S(1)} custom-call(bf16[3,256,512]{2,1,0:T(8,128)(2,1)} %forces.1, s32[1,256]{1,0:T(1,128)} %bitcast.9, bf16[2,3,32,256]{3,2,1,0:T(8,128)(2,1)} %bitcast.8, bf16[2,768,768]{2,1,0:T(8,128)(2,1)} %bitcast.5, s32[1,2]{1,0:T(1,128)} %near_col_hbm.1, bf16[512,768]{1,0:T(8,128)(2,1)} %bitcast.6, ...), custom_call_target="tpu_custom_call" | custom-call | tf_op jit(solution)/shard_map/pallas_call | solution.py:470
  34.7 0.7 %copy.12 = f32[3,256,128]{2,1,0:T(8,128)} copy(f32[3,256,128]{2,1,0:T(8,128)S(1)} %shard_map.100) | data formatting | bytes 786432

commit v4 on v3

--- a/solution.py
+++ b/solution.py
@@ -12,15 +12,29 @@
 SENDS = 48
 
 
-def kernel(
+def kernel(n, groups, levels, rank, comps, *refs):
+    dma = pltpu.SemaphoreType.DMA
+
+    def scoped(*sems):
+        body(n, groups, levels, rank, comps, *sems, *refs)
+
+    pl.run_scoped(
+        scoped,
+        dma((9,)), dma((groups,)), dma((SENDS,)), dma((n // 2,)),
+        dma((5,)), dma((groups,)), dma((groups, comps + 1, 2)), dma((groups, comps + 1)), dma((groups,)), dma((1,)),
+        dma((1,)), dma((n // 2,)), dma((1,)), dma((2, groups)), dma((groups, 2)), dma((2,)),
+    )
+
+
+def body(
     n, groups, levels, rank, comps,
+    local_sem, own_sem, send_sem, piece_send, order_recv, mate_recv, z_recv, across_recv, ext_recv, near_recv,
+    pair_recv, piece_recv, table_recv, w_recv, y_recv, mid_recv,
     forces, order_hbm, bases_hbm, tiles_hbm, near_col_hbm, basis_hbm, coupling_hbm, scale_hbm, ranks_hbm, targets_hbm,
     out,
     order, bases, coupling, near_col, scale, ranks, targets, tiles, basis,
     ext_out, ext_near, orders, spread, picks, own_pick, piece_out, piece_mate, pieces,
-    table, w_out, w_in, w_own, w_all, y_out, y_in, y_mid, totals, pair_total,
-    local_sem, own_sem, send_sem, piece_send, order_recv, mate_recv, z_recv, across_recv, ext_recv, near_recv,
-    pair_recv, piece_recv, table_recv, w_recv, y_recv, mid_recv,
+    table, w_out, w_in, w_own, w_low, w_all, y_out, y_in, y_mid, totals, pair_total,
     *blocks,
 ):
     g, c = lax.axis_index("grp"), lax.axis_index("clu")
@@ -71,19 +85,25 @@
     def columns_of(i, d):
         return forces.at[d, :, pl.ds(pl.multiple_of(partners[i] * width, width), width)]
 
-    def part(i, p, d):
+    def place_of(i, p, d, lo=0, hi=tile):
         if i == 0:
-            return own_blocks[d].at[p]
+            return own_blocks[d].at[p, lo:hi]
         if i == last:
-            return far_blocks[d].at[p]
-        return side_blocks[d].at[p, :, pl.ds((i - 1) * width, width)]
+            return far_blocks[d].at[p, lo:hi]
+        return side_blocks[d].at[p, lo:hi, pl.ds((i - 1) * width, width)]
+
+    chunks = [(d, 0, tile) for d in range(comps - 1)]
+    chunks += [(comps - 1, 0, tile // 2), (comps - 1, tile // 2, tile)]
+    parts = range(len(chunks))
+
+    def part(i, p, k):
+        return place_of(i, p, *chunks[k])
+
+    def part_bytes(k, count):
+        return own_blocks[0].at[0:count, 0:chunks[k][2] - chunks[k][1]]
 
     def edge_rows(i, p, d):
-        if i == 0:
-            return own_blocks[d].at[p, 0:quarter]
-        if i == last:
-            return far_blocks[d].at[p, 0:quarter]
-        return side_blocks[d].at[p, 0:quarter, pl.ds((i - 1) * width, width)]
+        return place_of(i, p, d, 0, quarter)
 
     small = [
         pltpu.make_async_copy(src, dst, local_sem.at[at])
@@ -96,7 +116,7 @@
         copy.start()
     for i in (last, 0, 1, 2):
         for d in range(comps):
-            pltpu.make_async_copy(columns_of(i, d), part(i, 3 + core, d), own_sem.at[i]).start()
+            pltpu.make_async_copy(columns_of(i, d), place_of(i, 3 + core, d), own_sem.at[i]).start()
     for copy in small[6:]:
         copy.start()
 
@@ -178,21 +198,27 @@
     for by in (-1, 1, -2, 2):
         push([(order, orders.at[2 - by], order_recv.at[2 - by], at_clu(by))], order)
 
-    def z_copies(i, d):
-        return [
-            (part(i, 3 + core, d), part(i, 1 + core, d), z_recv.at[i, d, 0], at_clu(2)),
-            (part(i, 3 + core, d), part(i, 5 + core, d), z_recv.at[i, d, 1], at_clu(-2)),
-        ]
-
-    for d in range(comps - 1):
-        push(z_copies(last, d), several(2))
+    def send_z(i, k):
+        push(
+            [
+                (part(i, 3 + core, k), part(i, 1 + core, k), z_recv.at[i, k, 0], at_clu(2)),
+                (part(i, 3 + core, k), part(i, 5 + core, k), z_recv.at[i, k, 1], at_clu(-2)),
+            ],
+            part_bytes(k, 2),
+        )
+
+    for k in range(2):
+        send_z(last, k)
     push(
         [(w_out.at[partners[i]], w_in.at[i], w_recv.at[0, i], at_grp(i)) for i in range(1, groups)],
         w_out.at[0:groups - 1],
     )
 
     def send_mate(i):
-        push([(part(i, 3 + core, d), part(i, 3 + core, d), mate_recv.at[i], mate) for d in range(comps)], several(comps))
+        push(
+            [(place_of(i, 3 + core, d), place_of(i, 3 + core, d), mate_recv.at[i], mate) for d in range(comps)],
+            several(comps),
+        )
 
     send_mate(last)
     own_arrived(0)
@@ -222,11 +248,12 @@
         ],
         ext_out.at[1],
     )
-    push(z_copies(last, comps - 1), several(2))
+    for k in parts[2:]:
+        send_z(last, k)
     pick_edge(0, own_blocks)
     push([(ext_out.at[0], ext_near.at[:, 0:quarter], near_recv.at[0], at_clu(2 * core - 1))], ext_out.at[0])
-    for d in range(comps - 1):
-        push(z_copies(0, d), several(2))
+    for k in parts[:2]:
+        send_z(0, k)
     for i in (1, 2):
         own_arrived(i)
         send_mate(i)
@@ -251,18 +278,19 @@
 
         one_hot(spot, store_pick, picks.shape[2] // 128)
 
-    def relay(i, d):
+    def relay(i, k):
         copies = []
         for side, p in enumerate((1 + core, 5 + core)):
-            landed(part(i, p, d), z_recv.at[i, d, side])
-            copies.append((part(i, p, d), part(i, p, d), across_recv.at[i, d], mate))
+            landed(part(i, p, k), z_recv.at[i, k, side])
             if i == last:
                 for to, at in ((1, 2), (2, 1)):
-                    copies.append((part(i, p, d), part(at, p, d), z_recv.at[at, d, side], at_grp(to)))
-        push(copies, several(len(copies)))
-
-    def take(i, d):
-        landed(several(2), across_recv.at[i, d])
+                    copies.append((part(i, p, k), part(at, p, k), z_recv.at[at, k, side], at_grp(to)))
+            copies.append((part(i, p, k), part(i, p, k), across_recv.at[i, k], mate))
+        push(copies, part_bytes(k, len(copies)))
+
+    def take(i, *ks):
+        for k in ks:
+            landed(part_bytes(k, 2), across_recv.at[i, k])
 
     def near(block, d):
         acc = None
@@ -277,6 +305,16 @@
 
     relay(last, 0)
     relay(last, 1)
+    for i in range(1, groups):
+        landed(w_in.at[i], w_recv.at[0, i])
+    summed = w_out[g]
+    for i in range(1, groups):
+        summed = summed + w_in[i]
+    high = summed.astype(BF16)
+    w_own[...] = high
+    w_all[g] = high
+    w_low[...] = (summed - high.astype(F32)).astype(BF16)
+    relay(last, 2)
     landed(ext_out.at[1], ext_recv.at[last])
     push(
         [
@@ -285,26 +323,18 @@
         ],
         ext_out,
     )
+    relay(last, 3)
     landed(several(comps), mate_recv.at[last])
     small[8].wait()
     take(last, 0)
     totals[...] = near(far_blocks, 0)
-
-    for i in range(1, groups):
-        landed(w_in.at[i], w_recv.at[0, i])
-    summed = w_out[g]
-    for i in range(1, groups):
-        summed = summed + w_in[i]
-    w_own[...] = summed.astype(BF16)
-    w_all[g] = summed.astype(BF16)
-
-    relay(last, 2)
-    push([(w_own, w_all.at[g], w_recv.at[1, i], at_grp(i)) for i in range(1, groups)], w_all.at[0:groups - 1])
+    for i in (1, 2):
+        relay(i, 0)
     take(last, 1)
     totals[...] += near(far_blocks, 1)
     for i in (1, 2):
-        relay(i, 0)
-    take(last, 2)
+        relay(i, 1)
+    take(last, 2, 3)
     y_out[last] = (totals[...] + near(far_blocks, 2)).astype(BF16)
     push(
         [
@@ -313,9 +343,19 @@
         ],
         y_out.at[last],
     )
-
+    push([(w_own, w_all.at[g], w_recv.at[1, i], at_grp(i)) for i in range(1, groups)], w_all.at[0:groups - 1])
+
+    for i in (1, 2):
+        relay(i, 2)
     small[6].wait()
     landed(ext_out.at[0], near_recv.at[0])
+    push(
+        [
+            (ext_near.at[d, 0:quarter], edge_rows(0, edge, d), ext_recv.at[0], at_clu(2 - 4 * core))
+            for d in range(comps)
+        ],
+        ext_out.at[0],
+    )
     landed(several(comps), mate_recv.at[0])
     piece = jnp.zeros((2 * piece_rows, width), F32)
     for d in range(comps):
@@ -329,7 +369,7 @@
         piece_out[h] = piece[h * piece_rows:(h + 1) * piece_rows]
     push([(piece_out.at[1 - core], piece_mate, pair_recv.at[0], mate)], piece_mate)
     for i in (1, 2):
-        relay(i, 1)
+        relay(i, 3)
 
     landed(piece_mate, pair_recv.at[0])
     pair = piece_out[core] + piece_mate[...]
@@ -347,14 +387,8 @@
         return carry
 
     lax.fori_loop(1, half, start_piece, 0)
-    push(z_copies(0, comps - 1), several(2))
-    push(
-        [
-            (ext_near.at[d, 0:quarter], edge_rows(0, edge, d), ext_recv.at[0], at_clu(2 - 4 * core))
-            for d in range(comps)
-        ],
-        ext_out.at[0],
-    )
+    for k in parts[2:]:
+        send_z(0, k)
 
     for i in (1, 2):
         landed(several(comps), mate_recv.at[i])
@@ -362,13 +396,11 @@
         take(i, 0)
     pair_total[...] = near(side_blocks, 0)
     for i in (1, 2):
-        relay(i, 2)
-    for i in (1, 2):
         take(i, 1)
     pair_total[...] += near(side_blocks, 1)
     relay(0, 0)
     for i in (1, 2):
-        take(i, 2)
+        take(i, 2, 3)
     both = pair_total[...] + near(side_blocks, 2)
 
     def send_y(i, h, value):
@@ -386,6 +418,10 @@
     landed(y_mid.at[0], mid_recv.at[0])
     send_y(2, 0, half_of(2, 0) + y_mid[0].astype(F32))
     relay(0, 1)
+
+    landed(ext_out.at[0], ext_recv.at[0])
+    take(0, 0)
+    totals[...] = near(own_blocks, 0)
 
     def await_piece(d, carry):
         source = lax.rem(c // 2 + d, half)
@@ -409,9 +445,8 @@
             at += cut
     push([(table.at[core], table.at[core], table_recv.at[0], mate)], table.at[0])
 
-    landed(ext_out.at[0], ext_recv.at[0])
-    take(0, 0)
-    totals[...] = near(own_blocks, 0)
+    take(0, 1)
+    totals[...] += near(own_blocks, 1)
     relay(0, 2)
     for i in range(1, groups):
         landed(w_own, w_recv.at[1, i])
@@ -421,9 +456,11 @@
     low = (entries - high.astype(F32)).astype(BF16)
     weights = w_all[...].reshape(rows, 2 * table_rows)
     answer = jnp.dot(weights, high, preferred_element_type=F32) + jnp.dot(weights, low, preferred_element_type=F32)
-    take(0, 1)
-    totals[...] += answer + near(own_blocks, 1)
-    take(0, 2)
+    totals[...] += answer
+    own_rows = pl.ds(pl.multiple_of(g * (rows // groups), rows // groups), rows // groups)
+    totals[own_rows] += jnp.dot(w_low[...], high, preferred_element_type=F32)
+    relay(0, 3)
+    take(0, 2, 3)
     totals[...] += near(own_blocks, 2)
 
     for copy in sends:
@@ -454,7 +491,6 @@
         slots = 8
         pad = 128
         vmem, hbm = (pl.BlockSpec(memory_space=m) for m in (pltpu.VMEM, pl.ANY))
-        dma = pltpu.SemaphoreType.DMA
         operands = (
             forces,
             order.reshape(1, tile),
@@ -495,15 +531,13 @@
                 pltpu.VMEM((groups, rows // groups, 2 * table_rows), F32),
                 pltpu.VMEM((groups, rows // groups, 2 * table_rows), F32),
                 pltpu.VMEM((rows // groups, 2 * table_rows), BF16),
+                pltpu.VMEM((rows // groups, 2 * table_rows), BF16),
                 pltpu.VMEM((groups, rows // groups, 2 * table_rows), BF16),
                 pltpu.VMEM((groups, rows, width), BF16),
                 pltpu.VMEM((groups, rows, width), BF16),
                 pltpu.VMEM((2, rows // 2, width), BF16),
                 pltpu.VMEM((rows, width), F32),
                 pltpu.VMEM((rows, 2 * width), F32),
-                dma((9,)), dma((groups,)), dma((SENDS,)), dma((n // 2,)),
-                dma((5,)), dma((groups,)), dma((groups, comps, 2)), dma((groups, comps)), dma((groups,)), dma((1,)),
-                dma((1,)), dma((n // 2,)), dma((1,)), dma((2, groups)), dma((groups, 2)), dma((2,)),
                 *(pltpu.VMEM((slots, tile, size), BF16) for size in (width, width, 2 * width) for _ in range(comps)),
             ],
             compiler_params=pltpu.CompilerParams(

time: 35.6 us -> 33.2 us (0.933)
  Pallas kernels: 34.7 us -> 32.3 us
    pallas_call x1, Pallas kernels: 34.7 us -> 32.3 us  [on_device(): pl.pallas_call(functools.partial(kernel, n, groups, levels, rank, comps),...]
where the time goes in v4:
time: 33.2 us; the launch traced here: 33 us
  Pallas kernels  32.3 us (97%)
  local copies, waits for them, and re-layouts  0.75 us (2%)
    pallas_call x1, Pallas kernels, on_device(): pl.pallas_call(functools.partial(kernel, n, groups, levels, rank, comps),...  32.3 us
    unnamed x1, local copies, waits for them, and re-layouts  0.75 us

profile of v4, /device:TPU:0, one launch (start us, length us, event | category | flops | bytes accessed | tf_op | source)
XLA Modules:
  0.0 33.0 jit_solution(1461621662662818259)
XLA Ops:
  0.0 32.3 %shard_map.100 = f32[3,256,128]{2,1,0:T(8,128)S(1)} custom-call(bf16[3,256,512]{2,1,0:T(8,128)(2,1)} %refs_0_.1, s32[1,256]{1,0:T(1,128)} %bitcast.9, bf16[2,3,32,256]{3,2,1,0:T(8,128)(2,1)} %bitcast.8, bf16[2,768,768]{2,1,0:T(8,128)(2,1)} %bitcast.5, s32[1,2]{1,0:T(1,128)} %refs_4_.1, bf16[512,768]{1,0:T(8,128)(2,1)} %bitcast.6, bf16[512,32]{1,0:T(8,128)(2,1)} %bitcast.7, ...), custom_call_target="tpu_custom_call" | custom-call | tf_op jit(solution)/shard_map/pallas_call | solution.py:506
  32.3 0.7 %copy.12 = f32[3,256,128]{2,1,0:T(8,128)} copy(f32[3,256,128]{2,1,0:T(8,128)S(1)} %shard_map.100) | data formatting | bytes 786432

commit v5 on v4

--- a/solution.py
+++ b/solution.py
@@ -112,28 +112,71 @@
             (scale_hbm, scale), (basis_hbm, basis), (bases_hbm, bases), (near_col_hbm, near_col), (tiles_hbm, tiles),
         ))
     ]
-    for copy in small[:6]:
+    for d in range(comps):
+        pltpu.make_async_copy(columns_of(last, d), place_of(last, 3 + core, d), own_sem.at[last]).start()
+    small[0].start()
+
+    barrier = pltpu.get_barrier_semaphore()
+
+    def greet(d, carry):
+        pl.semaphore_signal(barrier, inc=1, device_id=at_clu(d), device_id_type=MESH)
+        return carry
+
+    lax.fori_loop(1, n, greet, 0)
+    for d in range(1, groups):
+        pl.semaphore_signal(barrier, inc=1, device_id=at_grp(d), device_id_type=MESH)
+
+    for copy in small[1:6]:
         copy.start()
-    for i in (last, 0, 1, 2):
+    for i in (0, 1, 2):
         for d in range(comps):
             pltpu.make_async_copy(columns_of(i, d), place_of(i, 3 + core, d), own_sem.at[i]).start()
     for copy in small[6:]:
         copy.start()
 
-    barrier = pltpu.get_barrier_semaphore()
-
-    def greet(d, carry):
-        pl.semaphore_signal(barrier, inc=1, device_id=at_clu(d), device_id_type=MESH)
-        return carry
-
-    lax.fori_loop(1, n, greet, 0)
-    for d in range(1, groups):
-        pl.semaphore_signal(barrier, inc=1, device_id=at_grp(d), device_id_type=MESH)
-
     for block in blocks:
         block[edge, quarter:, :] = jnp.zeros((tile - quarter, block.shape[2]), BF16)
     ext_near[:, quarter:, :] = jnp.zeros((comps, ext_near.shape[1] - quarter, width), BF16)
 
+    sub = lax.broadcasted_iota(jnp.int32, (tile, tile), 0)
+    lan = lax.broadcasted_iota(jnp.int32, (tile, tile), 1)
+    upto = (sub <= lan).astype(BF16)
+
+    def ranked(chosen):
+        spots = jnp.broadcast_to(chosen.astype(F32), (8, tile)).astype(BF16)
+        return (jnp.dot(spots, upto, preferred_element_type=F32)[0:1, :] - 1.0).astype(jnp.int32)
+
+    def wrapped(spot):
+        spot = jnp.where(spot < 0, spot + n * tile, spot)
+        return jnp.where(spot >= n * tile, spot - n * tile, spot)
+
+    def one_hot(spot, store, count):
+        down = jnp.broadcast_to(spot.astype(F32), (128, tile)).T
+        at = lax.broadcasted_iota(jnp.int32, (tile, 128), 1).astype(F32)
+        for j in range(count):
+            store(j, (down == at + float(j * 128)).astype(F32).astype(BF16))
+
+    def own_arrived(i):
+        pltpu.make_async_copy(several(comps), several(comps), own_sem.at[i]).wait()
+
+    small[0].wait()
+    own_arrived(last)
+    pl.semaphore_wait(barrier, n - 1 + groups - 1)
+
+    for by in (-1, 1, -2, 2):
+        push([(order, orders.at[2 - by], order_recv.at[2 - by], at_clu(by))], order)
+
+    def send_z(i, k):
+        push(
+            [
+                (part(i, 3 + core, k), part(i, 1 + core, k), z_recv.at[i, k, 0], at_clu(2)),
+                (part(i, 3 + core, k), part(i, 5 + core, k), z_recv.at[i, k, 1], at_clu(-2)),
+            ],
+            part_bytes(k, 2),
+        )
+
+    for k in range(2):
+        send_z(last, k)
     for copy in small[1:5]:
         copy.wait()
     lane = lax.broadcasted_iota(jnp.int32, (rank, 2 * table_rows), 1)
@@ -161,54 +204,6 @@
     folded = folded[:, :2 * table_rows] + folded[:, 2 * table_rows:]
     w_out[...] = folded.reshape(groups, rows // groups, 2 * table_rows)
 
-    sub = lax.broadcasted_iota(jnp.int32, (tile, tile), 0)
-    lan = lax.broadcasted_iota(jnp.int32, (tile, tile), 1)
-    upto = (sub <= lan).astype(BF16)
-
-    def ranked(chosen):
-        spots = jnp.broadcast_to(chosen.astype(F32), (8, tile)).astype(BF16)
-        return (jnp.dot(spots, upto, preferred_element_type=F32)[0:1, :] - 1.0).astype(jnp.int32)
-
-    def wrapped(spot):
-        spot = jnp.where(spot < 0, spot + n * tile, spot)
-        return jnp.where(spot >= n * tile, spot - n * tile, spot)
-
-    def one_hot(spot, store, count):
-        down = jnp.broadcast_to(spot.astype(F32), (128, tile)).T
-        at = lax.broadcasted_iota(jnp.int32, (tile, 128), 1).astype(F32)
-        for j in range(count):
-            store(j, (down == at + float(j * 128)).astype(F32).astype(BF16))
-
-    small[0].wait()
-    spot = wrapped(order[...] - (c - core) * tile)
-    beyond = spot >= 2 * tile
-    spot = jnp.where(beyond, 2 * tile + ranked(beyond), spot)
-
-    def store_own(j, value):
-        own_pick[:, j * 128:(j + 1) * 128] = value
-
-    one_hot(spot, store_own, own_pick.shape[1] // 128)
-
-    def own_arrived(i):
-        pltpu.make_async_copy(several(comps), several(comps), own_sem.at[i]).wait()
-
-    own_arrived(last)
-    pl.semaphore_wait(barrier, n - 1 + groups - 1)
-
-    for by in (-1, 1, -2, 2):
-        push([(order, orders.at[2 - by], order_recv.at[2 - by], at_clu(by))], order)
-
-    def send_z(i, k):
-        push(
-            [
-                (part(i, 3 + core, k), part(i, 1 + core, k), z_recv.at[i, k, 0], at_clu(2)),
-                (part(i, 3 + core, k), part(i, 5 + core, k), z_recv.at[i, k, 1], at_clu(-2)),
-            ],
-            part_bytes(k, 2),
-        )
-
-    for k in range(2):
-        send_z(last, k)
     push(
         [(w_out.at[partners[i]], w_in.at[i], w_recv.at[0, i], at_grp(i)) for i in range(1, groups)],
         w_out.at[0:groups - 1],
@@ -226,6 +221,15 @@
 
     def order_landed(by):
         landed(orders.at[2 + by], order_recv.at[2 + by])
+
+    spot = wrapped(order[...] - (c - core) * tile)
+    beyond = spot >= 2 * tile
+    spot = jnp.where(beyond, 2 * tile + ranked(beyond), spot)
+
+    def store_own(j, value):
+        own_pick[:, j * 128:(j + 1) * 128] = value
+
+    one_hot(spot, store_own, own_pick.shape[1] // 128)
 
     for by in (-1, 1):
         order_landed(by)
@@ -252,8 +256,6 @@
         send_z(last, k)
     pick_edge(0, own_blocks)
     push([(ext_out.at[0], ext_near.at[:, 0:quarter], near_recv.at[0], at_clu(2 * core - 1))], ext_out.at[0])
-    for k in parts[:2]:
-        send_z(0, k)
     for i in (1, 2):
         own_arrived(i)
         send_mate(i)
@@ -292,12 +294,19 @@
         for k in ks:
             landed(part_bytes(k, 2), across_recv.at[i, k])
 
-    def near(block, d):
+    def near(block, lo, hi):
         acc = None
         for j in range(near_count):
-            held = block[d][pl.ds(starts[j], 3)].reshape(3 * tile, block[d].shape[2])
-            x = jnp.dot(picks[j], held, preferred_element_type=F32).astype(BF16)
-            term = jnp.dot(tiles[j, :, d * tile:(d + 1) * tile], x, preferred_element_type=F32)
+            found = [
+                jnp.dot(
+                    picks[j], block[d][pl.ds(starts[j], 3)].reshape(3 * tile, block[d].shape[2]),
+                    preferred_element_type=F32,
+                ).astype(BF16)
+                for d in range(lo, hi)
+            ]
+            term = jnp.dot(
+                tiles[j, :, lo * tile:hi * tile], jnp.concatenate(found, axis=0), preferred_element_type=F32
+            )
             acc = term if acc is None else acc + term
         return acc
 
@@ -305,6 +314,7 @@
 
     relay(last, 0)
     relay(last, 1)
+    send_z(0, 0)
     for i in range(1, groups):
         landed(w_in.at[i], w_recv.at[0, i])
     summed = w_out[g]
@@ -315,6 +325,7 @@
     w_all[g] = high
     w_low[...] = (summed - high.astype(F32)).astype(BF16)
     relay(last, 2)
+    send_z(0, 1)
     landed(ext_out.at[1], ext_recv.at[last])
     push(
         [
@@ -323,19 +334,15 @@
         ],
         ext_out,
     )
-    relay(last, 3)
     landed(several(comps), mate_recv.at[last])
     small[8].wait()
-    take(last, 0)
-    totals[...] = near(far_blocks, 0)
+    take(last, 0, 1)
+    totals[...] = near(far_blocks, 0, comps - 1)
+    relay(last, 3)
     for i in (1, 2):
         relay(i, 0)
-    take(last, 1)
-    totals[...] += near(far_blocks, 1)
-    for i in (1, 2):
-        relay(i, 1)
     take(last, 2, 3)
-    y_out[last] = (totals[...] + near(far_blocks, 2)).astype(BF16)
+    y_out[last] = (totals[...] + near(far_blocks, comps - 1, comps)).astype(BF16)
     push(
         [
             (y_out.at[last, 0:mid], y_mid.at[0], mid_recv.at[0], at_grp(1)),
@@ -345,8 +352,9 @@
     )
     push([(w_own, w_all.at[g], w_recv.at[1, i], at_grp(i)) for i in range(1, groups)], w_all.at[0:groups - 1])
 
-    for i in (1, 2):
-        relay(i, 2)
+    for k in (1, 2):
+        for i in (1, 2):
+            relay(i, k)
     small[6].wait()
     landed(ext_out.at[0], near_recv.at[0])
     push(
@@ -393,15 +401,12 @@
     for i in (1, 2):
         landed(several(comps), mate_recv.at[i])
         landed(ext_out.at[0], ext_recv.at[i])
-        take(i, 0)
-    pair_total[...] = near(side_blocks, 0)
-    for i in (1, 2):
-        take(i, 1)
-    pair_total[...] += near(side_blocks, 1)
+        take(i, 0, 1)
+    pair_total[...] = near(side_blocks, 0, comps - 1)
     relay(0, 0)
     for i in (1, 2):
         take(i, 2, 3)
-    both = pair_total[...] + near(side_blocks, 2)
+    both = pair_total[...] + near(side_blocks, comps - 1, comps)
 
     def send_y(i, h, value):
         here = pl.ds(h * mid, mid)
@@ -421,7 +426,7 @@
 
     landed(ext_out.at[0], ext_recv.at[0])
     take(0, 0)
-    totals[...] = near(own_blocks, 0)
+    totals[...] = near(own_blocks, 0, 1)
 
     def await_piece(d, carry):
         source = lax.rem(c // 2 + d, half)
@@ -446,7 +451,7 @@
     push([(table.at[core], table.at[core], table_recv.at[0], mate)], table.at[0])
 
     take(0, 1)
-    totals[...] += near(own_blocks, 1)
+    totals[...] += near(own_blocks, 1, 2)
     relay(0, 2)
     for i in range(1, groups):
         landed(w_own, w_recv.at[1, i])
@@ -461,7 +466,7 @@
     totals[own_rows] += jnp.dot(w_low[...], high, preferred_element_type=F32)
     relay(0, 3)
     take(0, 2, 3)
-    totals[...] += near(own_blocks, 2)
+    totals[...] += near(own_blocks, comps - 1, comps)
 
     for copy in sends:
         copy.wait_send()

time: 33.2 us -> 32.4 us (0.976)
  Pallas kernels: 32.3 us -> 31.5 us
    pallas_call x1, Pallas kernels: 32.3 us -> 31.5 us  [on_device(): pl.pallas_call(functools.partial(kernel, n, groups, levels, rank, comps),...]
where the time goes in v5:
time: 32.4 us; the launch traced here: 32.3 us
  Pallas kernels  31.5 us (97%)
  local copies, waits for them, and re-layouts  0.75 us (2%)
    pallas_call x1, Pallas kernels, on_device(): pl.pallas_call(functools.partial(kernel, n, groups, levels, rank, comps),...  31.5 us
    unnamed x1, local copies, waits for them, and re-layouts  0.75 us

profile of v5, /device:TPU:0, one launch (start us, length us, event | category | flops | bytes accessed | tf_op | source)
XLA Modules:
  0.0 32.3 jit_solution(15752994610016815237)
XLA Ops:
  0.0 31.5 %shard_map.100 = f32[3,256,128]{2,1,0:T(8,128)S(1)} custom-call(bf16[3,256,512]{2,1,0:T(8,128)(2,1)} %refs_0_.1, s32[1,256]{1,0:T(1,128)} %bitcast.9, bf16[2,3,32,256]{3,2,1,0:T(8,128)(2,1)} %bitcast.8, bf16[2,768,768]{2,1,0:T(8,128)(2,1)} %bitcast.5, s32[1,2]{1,0:T(1,128)} %refs_4_.1, bf16[512,768]{1,0:T(8,128)(2,1)} %bitcast.6, bf16[512,32]{1,0:T(8,128)(2,1)} %bitcast.7, ...), custom_call_target="tpu_custom_call" | custom-call | tf_op jit(solution)/shard_map/pallas_call | solution.py:511
  31.5 0.7 %copy.12 = f32[3,256,128]{2,1,0:T(8,128)} copy(f32[3,256,128]{2,1,0:T(8,128)S(1)} %shard_map.100) | data formatting | bytes 786432

commit v6 on v4

--- a/solution.py
+++ b/solution.py
@@ -179,19 +179,10 @@
         for j in range(count):
             store(j, (down == at + float(j * 128)).astype(F32).astype(BF16))
 
-    small[0].wait()
-    spot = wrapped(order[...] - (c - core) * tile)
-    beyond = spot >= 2 * tile
-    spot = jnp.where(beyond, 2 * tile + ranked(beyond), spot)
-
-    def store_own(j, value):
-        own_pick[:, j * 128:(j + 1) * 128] = value
-
-    one_hot(spot, store_own, own_pick.shape[1] // 128)
-
     def own_arrived(i):
         pltpu.make_async_copy(several(comps), several(comps), own_sem.at[i]).wait()
 
+    small[0].wait()
     own_arrived(last)
     pl.semaphore_wait(barrier, n - 1 + groups - 1)
 
@@ -227,6 +218,15 @@
     def order_landed(by):
         landed(orders.at[2 + by], order_recv.at[2 + by])
 
+    spot = wrapped(order[...] - (c - core) * tile)
+    beyond = spot >= 2 * tile
+    spot = jnp.where(beyond, 2 * tile + ranked(beyond), spot)
+
+    def store_own(j, value):
+        own_pick[:, j * 128:(j + 1) * 128] = value
+
+    one_hot(spot, store_own, own_pick.shape[1] // 128)
+
     for by in (-1, 1):
         order_landed(by)
     away = orders[1 + 2 * core] - c * tile
@@ -240,6 +240,8 @@
         for d in range(comps):
             ext_out[at, d] = jnp.dot(pick, own[d][3 + core], preferred_element_type=F32).astype(BF16)[:quarter]
 
+    for k in parts[2:]:
+        send_z(last, k)
     pick_edge(1, far_blocks)
     push(
         [
@@ -248,12 +250,7 @@
         ],
         ext_out.at[1],
     )
-    for k in parts[2:]:
-        send_z(last, k)
     pick_edge(0, own_blocks)
-    push([(ext_out.at[0], ext_near.at[:, 0:quarter], near_recv.at[0], at_clu(2 * core - 1))], ext_out.at[0])
-    for k in parts[:2]:
-        send_z(0, k)
     for i in (1, 2):
         own_arrived(i)
         send_mate(i)
@@ -292,12 +289,19 @@
         for k in ks:
             landed(part_bytes(k, 2), across_recv.at[i, k])
 
-    def near(block, d):
+    def near(block, lo, hi):
         acc = None
         for j in range(near_count):
-            held = block[d][pl.ds(starts[j], 3)].reshape(3 * tile, block[d].shape[2])
-            x = jnp.dot(picks[j], held, preferred_element_type=F32).astype(BF16)
-            term = jnp.dot(tiles[j, :, d * tile:(d + 1) * tile], x, preferred_element_type=F32)
+            found = [
+                jnp.dot(
+                    picks[j], block[d][pl.ds(starts[j], 3)].reshape(3 * tile, block[d].shape[2]),
+                    preferred_element_type=F32,
+                ).astype(BF16)
+                for d in range(lo, hi)
+            ]
+            term = jnp.dot(
+                tiles[j, :, lo * tile:hi * tile], jnp.concatenate(found, axis=0), preferred_element_type=F32
+            )
             acc = term if acc is None else acc + term
         return acc
 
@@ -305,6 +309,7 @@
 
     relay(last, 0)
     relay(last, 1)
+    push([(ext_out.at[0], ext_near.at[:, 0:quarter], near_recv.at[0], at_clu(2 * core - 1))], ext_out.at[0])
     for i in range(1, groups):
         landed(w_in.at[i], w_recv.at[0, i])
     summed = w_out[g]
@@ -315,6 +320,11 @@
     w_all[g] = high
     w_low[...] = (summed - high.astype(F32)).astype(BF16)
     relay(last, 2)
+    relay(last, 3)
+    for k in parts[:2]:
+        send_z(0, k)
+    for i in (1, 2):
+        relay(i, 0)
     landed(ext_out.at[1], ext_recv.at[last])
     push(
         [
@@ -323,19 +333,10 @@
         ],
         ext_out,
     )
-    relay(last, 3)
     landed(several(comps), mate_recv.at[last])
     small[8].wait()
-    take(last, 0)
-    totals[...] = near(far_blocks, 0)
-    for i in (1, 2):
-        relay(i, 0)
-    take(last, 1)
-    totals[...] += near(far_blocks, 1)
-    for i in (1, 2):
-        relay(i, 1)
-    take(last, 2, 3)
-    y_out[last] = (totals[...] + near(far_blocks, 2)).astype(BF16)
+    take(last, 0, 1, 2, 3)
+    y_out[last] = near(far_blocks, 0, comps).astype(BF16)
     push(
         [
             (y_out.at[last, 0:mid], y_mid.at[0], mid_recv.at[0], at_grp(1)),
@@ -345,8 +346,9 @@
     )
     push([(w_own, w_all.at[g], w_recv.at[1, i], at_grp(i)) for i in range(1, groups)], w_all.at[0:groups - 1])
 
-    for i in (1, 2):
-        relay(i, 2)
+    for k in (1, 2):
+        for i in (1, 2):
+            relay(i, k)
     small[6].wait()
     landed(ext_out.at[0], near_recv.at[0])
     push(
@@ -393,15 +395,8 @@
     for i in (1, 2):
         landed(several(comps), mate_recv.at[i])
         landed(ext_out.at[0], ext_recv.at[i])
-        take(i, 0)
-    pair_total[...] = near(side_blocks, 0)
-    for i in (1, 2):
-        take(i, 1)
-    pair_total[...] += near(side_blocks, 1)
-    relay(0, 0)
-    for i in (1, 2):
-        take(i, 2, 3)
-    both = pair_total[...] + near(side_blocks, 2)
+        take(i, 0, 1, 2, 3)
+    both = near(side_blocks, 0, comps)
 
     def send_y(i, h, value):
         here = pl.ds(h * mid, mid)
@@ -417,11 +412,12 @@
     send_y(1, 1, half_of(1, 1) + y_mid[1].astype(F32))
     landed(y_mid.at[0], mid_recv.at[0])
     send_y(2, 0, half_of(2, 0) + y_mid[0].astype(F32))
+    relay(0, 0)
     relay(0, 1)
 
     landed(ext_out.at[0], ext_recv.at[0])
     take(0, 0)
-    totals[...] = near(own_blocks, 0)
+    totals[...] = near(own_blocks, 0, 1)
 
     def await_piece(d, carry):
         source = lax.rem(c // 2 + d, half)
@@ -446,7 +442,7 @@
     push([(table.at[core], table.at[core], table_recv.at[0], mate)], table.at[0])
 
     take(0, 1)
-    totals[...] += near(own_blocks, 1)
+    totals[...] += near(own_blocks, 1, 2)
     relay(0, 2)
     for i in range(1, groups):
         landed(w_own, w_recv.at[1, i])
@@ -461,7 +457,7 @@
     totals[own_rows] += jnp.dot(w_low[...], high, preferred_element_type=F32)
     relay(0, 3)
     take(0, 2, 3)
-    totals[...] += near(own_blocks, 2)
+    totals[...] += near(own_blocks, comps - 1, comps)
 
     for copy in sends:
         copy.wait_send()

time: 33.2 us -> 31.9 us (0.961)
  Pallas kernels: 32.3 us -> 31 us
    pallas_call x1, Pallas kernels: 32.3 us -> 31 us  [on_device(): pl.pallas_call(functools.partial(kernel, n, groups, levels, rank, comps),...]
where the time goes in v6:
time: 31.9 us; the launch traced here: 31.8 us
  Pallas kernels  31 us (97%)
  local copies, waits for them, and re-layouts  0.75 us (2%)
    pallas_call x1, Pallas kernels, on_device(): pl.pallas_call(functools.partial(kernel, n, groups, levels, rank, comps),...  31 us
    unnamed x1, local copies, waits for them, and re-layouts  0.75 us

profile of v6, /device:TPU:0, one launch (start us, length us, event | category | flops | bytes accessed | tf_op | source)
XLA Modules:
  0.0 31.8 jit_solution(7553521974941868746)
XLA Ops:
  0.0 31.0 %shard_map.100 = f32[3,256,128]{2,1,0:T(8,128)S(1)} custom-call(bf16[3,256,512]{2,1,0:T(8,128)(2,1)} %refs_0_.1, s32[1,256]{1,0:T(1,128)} %bitcast.9, bf16[2,3,32,256]{3,2,1,0:T(8,128)(2,1)} %bitcast.8, bf16[2,768,768]{2,1,0:T(8,128)(2,1)} %bitcast.5, s32[1,2]{1,0:T(1,128)} %refs_4_.1, bf16[512,768]{1,0:T(8,128)(2,1)} %bitcast.6, bf16[512,32]{1,0:T(8,128)(2,1)} %bitcast.7, ...), custom_call_target="tpu_custom_call" | custom-call | tf_op jit(solution)/shard_map/pallas_call | solution.py:502
  31.0 0.7 %copy.12 = f32[3,256,128]{2,1,0:T(8,128)} copy(f32[3,256,128]{2,1,0:T(8,128)S(1)} %shard_map.100) | data formatting | bytes 786432

commit v7 on v6

--- a/solution.py
+++ b/solution.py
@@ -289,21 +289,28 @@
         for k in ks:
             landed(part_bytes(k, 2), across_recv.at[i, k])
 
-    def near(block, lo, hi):
-        acc = None
+    def gathered(block, lo, hi):
+        found = []
         for j in range(near_count):
-            found = [
+            parts_of = [
                 jnp.dot(
                     picks[j], block[d][pl.ds(starts[j], 3)].reshape(3 * tile, block[d].shape[2]),
                     preferred_element_type=F32,
                 ).astype(BF16)
                 for d in range(lo, hi)
             ]
-            term = jnp.dot(
-                tiles[j, :, lo * tile:hi * tile], jnp.concatenate(found, axis=0), preferred_element_type=F32
-            )
+            found.append(jnp.concatenate(parts_of, axis=0))
+        return found
+
+    def product(found, lo, hi, top, bottom):
+        acc = None
+        for j in range(near_count):
+            term = jnp.dot(tiles[j, top:bottom, lo * tile:hi * tile], found[j], preferred_element_type=F32)
             acc = term if acc is None else acc + term
         return acc
+
+    def near(block, lo, hi):
+        return product(gathered(block, lo, hi), lo, hi, 0, rows)
 
     mid = rows // 2
 
@@ -396,22 +403,18 @@
         landed(several(comps), mate_recv.at[i])
         landed(ext_out.at[0], ext_recv.at[i])
         take(i, 0, 1, 2, 3)
-    both = near(side_blocks, 0, comps)
+    found = gathered(side_blocks, 0, comps)
 
     def send_y(i, h, value):
         here = pl.ds(h * mid, mid)
         y_out[i, h * mid:(h + 1) * mid] = value.astype(BF16)
         push([(y_out.at[i, here], y_in.at[i, here], y_recv.at[i, h], at_grp(i))], y_mid.at[0])
 
-    def half_of(i, h):
-        return both[h * mid:(h + 1) * mid, (i - 1) * width:i * width]
-
-    send_y(1, 0, half_of(1, 0))
-    send_y(2, 1, half_of(2, 1))
-    landed(y_mid.at[1], mid_recv.at[1])
-    send_y(1, 1, half_of(1, 1) + y_mid[1].astype(F32))
-    landed(y_mid.at[0], mid_recv.at[0])
-    send_y(2, 0, half_of(2, 0) + y_mid[0].astype(F32))
+    for h, plain, added in ((0, 1, 2), (1, 2, 1)):
+        both = product(found, 0, comps, h * mid, (h + 1) * mid)
+        send_y(plain, h, both[:, (plain - 1) * width:plain * width])
+        landed(y_mid.at[h], mid_recv.at[h])
+        send_y(added, h, both[:, (added - 1) * width:added * width] + y_mid[h].astype(F32))
     relay(0, 0)
     relay(0, 1)
 

time: 31.9 us -> 31.7 us (level)
  no operation moved by 1% of the time
where the time goes in v7:
time: 31.7 us; the launch traced here: 31.6 us
  Pallas kernels  30.9 us (97%)
  local copies, waits for them, and re-layouts  0.75 us (2%)
    pallas_call x1, Pallas kernels, on_device(): pl.pallas_call(functools.partial(kernel, n, groups, levels, rank, comps),...  30.9 us
    unnamed x1, local copies, waits for them, and re-layouts  0.75 us

profile of v7, /device:TPU:0, one launch (start us, length us, event | category | flops | bytes accessed | tf_op | source)
XLA Modules:
  0.0 31.6 jit_solution(12054388106588484433)
XLA Ops:
  0.0 30.9 %shard_map.100 = f32[3,256,128]{2,1,0:T(8,128)S(1)} custom-call(bf16[3,256,512]{2,1,0:T(8,128)(2,1)} %refs_0_.1, s32[1,256]{1,0:T(1,128)} %bitcast.9, bf16[2,3,32,256]{3,2,1,0:T(8,128)(2,1)} %bitcast.8, bf16[2,768,768]{2,1,0:T(8,128)(2,1)} %bitcast.5, s32[1,2]{1,0:T(1,128)} %refs_4_.1, bf16[512,768]{1,0:T(8,128)(2,1)} %bitcast.6, bf16[512,32]{1,0:T(8,128)(2,1)} %bitcast.7, ...), custom_call_target="tpu_custom_call" | custom-call | tf_op jit(solution)/shard_map/pallas_call | solution.py:505
  30.9 0.7 %copy.12 = f32[3,256,128]{2,1,0:T(8,128)} copy(f32[3,256,128]{2,1,0:T(8,128)S(1)} %shard_map.100) | data formatting | bytes 786432

commit v8 on v7

--- a/solution.py
+++ b/solution.py
@@ -53,6 +53,7 @@
     last = groups - 1
     own_blocks, far_blocks, side_blocks = (blocks[at * comps:(at + 1) * comps] for at in range(3))
     edge = 7 * core
+    flip = 1 - jnp.minimum(c // 2, 1)
 
     def at_clu(by):
         return {"grp": g, "clu": lax.rem(c + by + n, n)}
@@ -192,8 +193,11 @@
     def send_z(i, k):
         push(
             [
-                (part(i, 3 + core, k), part(i, 1 + core, k), z_recv.at[i, k, 0], at_clu(2)),
-                (part(i, 3 + core, k), part(i, 5 + core, k), z_recv.at[i, k, 1], at_clu(-2)),
+                (
+                    part(i, 3 + core, k), part(i, 1 + core + 4 * side, k), z_recv.at[i, k, side],
+                    at_clu(2 - 4 * side),
+                )
+                for side in (flip, 1 - flip)
             ],
             part_bytes(k, 2),
         )

time: 31.7 us -> 31.8 us (level)
  no operation moved by 1% of the time
where the time goes in v8:
time: 31.8 us; the launch traced here: 31.6 us
  Pallas kernels  30.9 us (97%)
  local copies, waits for them, and re-layouts  0.75 us (2%)
    pallas_call x1, Pallas kernels, on_device(): pl.pallas_call(functools.partial(kernel, n, groups, levels, rank, comps),...  30.9 us
    unnamed x1, local copies, waits for them, and re-layouts  0.75 us

profile of v8, /device:TPU:0, one launch (start us, length us, event | category | flops | bytes accessed | tf_op | source)
XLA Modules:
  0.0 31.6 jit_solution(2094038247650705564)
XLA Ops:
  0.0 30.9 %shard_map.100 = f32[3,256,128]{2,1,0:T(8,128)S(1)} custom-call(bf16[3,256,512]{2,1,0:T(8,128)(2,1)} %refs_0_.1, s32[1,256]{1,0:T(1,128)} %bitcast.9, bf16[2,3,32,256]{3,2,1,0:T(8,128)(2,1)} %bitcast.8, bf16[2,768,768]{2,1,0:T(8,128)(2,1)} %bitcast.5, s32[1,2]{1,0:T(1,128)} %refs_4_.1, bf16[512,768]{1,0:T(8,128)(2,1)} %bitcast.6, bf16[512,32]{1,0:T(8,128)(2,1)} %bitcast.7, ...), custom_call_target="tpu_custom_call" | custom-call | tf_op jit(solution)/shard_map/pallas_call | solution.py:509
  30.9 0.7 %copy.12 = f32[3,256,128]{2,1,0:T(8,128)} copy(f32[3,256,128]{2,1,0:T(8,128)S(1)} %shard_map.100) | data formatting | bytes 786432

commit v9 on v8

--- a/solution.py
+++ b/solution.py
@@ -370,14 +370,19 @@
         ext_out.at[0],
     )
     landed(several(comps), mate_recv.at[0])
-    piece = jnp.zeros((2 * piece_rows, width), F32)
-    for d in range(comps):
-        x = jnp.dot(own_pick[:, :2 * tile], own_blocks[d][3:5].reshape(2 * tile, width), preferred_element_type=F32)
-        x = x + jnp.dot(own_pick[:, 2 * tile:], ext_near[d], preferred_element_type=F32)
-        weights = jnp.concatenate(
-            [bases[level, d, h * cut:(h + 1) * cut] for h in range(2) for level in range(levels)], axis=0
-        )
-        piece = piece + jnp.dot(weights, x.astype(BF16), preferred_element_type=F32)
+    chip = jnp.concatenate([own_blocks[d][3:5].reshape(2 * tile, width) for d in range(comps)], axis=1)
+    near_edge = jnp.concatenate([ext_near[d] for d in range(comps)], axis=1)
+    x = jnp.dot(own_pick[:, :2 * tile], chip, preferred_element_type=F32)
+    x = (x + jnp.dot(own_pick[:, 2 * tile:], near_edge, preferred_element_type=F32)).astype(BF16)
+    stacked = jnp.concatenate([x[:, d * width:(d + 1) * width] for d in range(comps)], axis=0)
+    weights = jnp.concatenate(
+        [
+            jnp.concatenate([bases[level, d, h * cut:(h + 1) * cut] for d in range(comps)], axis=1)
+            for h in range(2) for level in range(levels)
+        ],
+        axis=0,
+    )
+    piece = jnp.dot(weights, stacked, preferred_element_type=F32)
     for h in range(2):
         piece_out[h] = piece[h * piece_rows:(h + 1) * piece_rows]
     push([(piece_out.at[1 - core], piece_mate, pair_recv.at[0], mate)], piece_mate)
@@ -463,9 +468,6 @@
     own_rows = pl.ds(pl.multiple_of(g * (rows // groups), rows // groups), rows // groups)
     totals[own_rows] += jnp.dot(w_low[...], high, preferred_element_type=F32)
     relay(0, 3)
-    take(0, 2, 3)
-    totals[...] += near(own_blocks, comps - 1, comps)
-
     for copy in sends:
         copy.wait_send()
 
@@ -474,6 +476,10 @@
         return carry
 
     lax.fori_loop(1, half, end_piece, 0)
+
+    take(0, 2, 3)
+    totals[...] += near(own_blocks, comps - 1, comps)
+
     for i in (1, 2):
         for h in range(2):
             landed(y_mid.at[0], y_recv.at[i, h])

time: 31.8 us -> 31.9 us (level)
  no operation moved by 1% of the time
where the time goes in v9:
time: 31.9 us; the launch traced here: 31.7 us
  Pallas kernels  31 us (97%)
  local copies, waits for them, and re-layouts  0.75 us (2%)
    pallas_call x1, Pallas kernels, on_device(): pl.pallas_call(functools.partial(kernel, n, groups, levels, rank, comps),...  31 us
    unnamed x1, local copies, waits for them, and re-layouts  0.75 us

profile of v9, /device:TPU:0, one launch (start us, length us, event | category | flops | bytes accessed | tf_op | source)
XLA Modules:
  0.0 31.7 jit_solution(1847955317933513207)
XLA Ops:
  0.0 31.0 %shard_map.100 = f32[3,256,128]{2,1,0:T(8,128)S(1)} custom-call(bf16[3,256,512]{2,1,0:T(8,128)(2,1)} %refs_0_.1, s32[1,256]{1,0:T(1,128)} %bitcast.9, bf16[2,3,32,256]{3,2,1,0:T(8,128)(2,1)} %bitcast.8, bf16[2,768,768]{2,1,0:T(8,128)(2,1)} %bitcast.5, s32[1,2]{1,0:T(1,128)} %refs_4_.1, bf16[512,768]{1,0:T(8,128)(2,1)} %bitcast.6, bf16[512,32]{1,0:T(8,128)(2,1)} %bitcast.7, ...), custom_call_target="tpu_custom_call" | custom-call | tf_op jit(solution)/shard_map/pallas_call | solution.py:515
  31.0 0.7 %copy.12 = f32[3,256,128]{2,1,0:T(8,128)} copy(f32[3,256,128]{2,1,0:T(8,128)S(1)} %shard_map.100) | data formatting | bytes 786432
